TPU v7x, 32 devices: a whole 2x2x4 slice. The times are simulated.
32 devices in a mesh: dom: 8 (over z, x), dir: 4 (over y, core).
Axes of the slice: x: 2, y: 2, z: 4, core: 2. Of those that a mesh axis runs over, the one named last changes fastest.
Arguments:
- x_edges: bfloat16 [65536, 128], P(('dom', 'dir')), may hold values from -6 to 6
- send_list: int32 [1024, 32], P(('dom', 'dir')), may hold values from 0 to 2048, as said below
- connectivity: int32 [6, 32768], P(None, ('dom', 'dir')), may hold values from 0 to 3071, as said below
- elem_mats: float32 [36, 32768], P(None, ('dom', 'dir'))
- elem_live: int32 [32], P(('dom', 'dir')), may hold values from 512 to 1024, as said below
- currents: bfloat16 [1024, 128, 128], P(('dom', 'dir')), may hold values from -0.1796875 to 0.1796875
- positions: bfloat16 [1024, 3, 128], P(('dom', 'dir')), may hold values from -1 to 1
- block_live: int32 [1024], P(('dom', 'dir')), may hold values from 32 to 128
- block_owner: int32 [1024], P(('dom', 'dir')), may hold values from 0 to 7, as said below
- block_leaf: int32 [1024], P(('dom', 'dir')), may hold values from 0 to 15
- cone_waves: float32 [3, 16], P(None, 'dir'), may hold values from -6 to 6
Outputs:
- interior_out: float32 [65536, 128], P(('dom', 'dir'))
- expansions: float32 [16, 16, 2, 64, 128], P('dom', 'dir')
Inputs may be any that keep to these rules, and one draw needn't show every extreme that they name: `send_list`: in row a * 32 + b the used entries come first and name owned edges of a; the rest are 2048. A partition reads nothing of itself; some pair uses all 32 entries. `connectivity`: entries below 2048 are owned edges; 2048 + p * 32 + s names the s-th edge that partition p lists for this partition, and only used entries are named. `elem_live`: elements at positions from this count on are padding; some partition has all 1024. `block_owner`: among the 32 blocks of one partition at most 12 name one leaf owner; some leaf owner is named by exactly 12 blocks of every partition.
All inputs are finite; a program needn't handle non-finite values.
Results may differ from a plain program's by a relative error of at most 0.0056.
Values may be sent and summed in bfloat16 or wider, within the bound.
A program may use at most 128 MiB of HBM per device.

v0:
```python
import jax
import jax.numpy as jnp
from jax import lax
from jax.experimental import pallas as pl
from jax.experimental.pallas import tpu as pltpu
from jax.sharding import PartitionSpec as P

LEAVES_DEV = 16
NODES = 4


def cheb_points():
    node_order = jnp.arange(NODES).astype(jnp.float32)
    return jnp.cos((2.0 * node_order + 1.0) * (jnp.pi / (2.0 * NODES)))


def lagrange(points):
    node_values = cheb_points()
    rows_out = []
    for target in range(NODES):
        product = jnp.ones_like(points)
        for other_node in range(NODES):
            if other_node != target:
                product = (
                    product
                    * (points - node_values[other_node])
                    / (node_values[target] - node_values[other_node])
                )
        rows_out.append(product)
    return jnp.stack(rows_out, axis=-2)


def tensor_basis(coords):
    first = lagrange(coords[..., 0, :])
    second = lagrange(coords[..., 1, :])
    third = lagrange(coords[..., 2, :])
    joined = (
        first[..., :, None, None, :] * second[..., None, :, None, :] * third[..., None, None, :, :]
    )
    return joined.reshape(coords.shape[:-2] + (NODES**3, coords.shape[-1]))


def node_coords():
    ladder = jnp.arange(NODES**3)
    digits = jnp.stack([ladder // (NODES * NODES), ladder // NODES % NODES, ladder % NODES]).astype(
        jnp.float32
    )
    return jnp.cos((2.0 * digits + 1.0) * (jnp.pi / (2.0 * NODES)))


def wave_phase(waves, coords):
    return (
        waves[0][:, None] * coords[..., None, 0, :]
        + waves[1][:, None] * coords[..., None, 1, :]
        + waves[2][:, None] * coords[..., None, 2, :]
    )


def m2m_tables(waves):
    octant = jnp.arange(8)
    shifts = jnp.stack([octant // 4, octant // 2 % 2, octant % 2], axis=1).astype(jnp.float32) - 0.5
    points = shifts[:, :, None] + 0.5 * cheb_points()[None, None, :]
    weights = lagrange(points)
    first = weights[:, 0]
    second = weights[:, 1]
    third = weights[:, 2]
    joined = (
        first[:, :, None, None, :, None, None]
        * second[:, None, :, None, None, :, None]
        * third[:, None, None, :, None, None, :]
    )
    square = NODES**3
    joined = joined.reshape(8, square, square)
    child = shifts[:, :, None] + 0.5 * node_coords()[None]
    spread = child[:, :, None, :] - node_coords()[None, :, :, None]
    psi = 2.0 * (
        waves[0][:, None, None, None] * spread[None, :, 0]
        + waves[1][:, None, None, None] * spread[None, :, 1]
        + waves[2][:, None, None, None] * spread[None, :, 2]
    )
    table_real = (joined[None] * jnp.cos(psi)).astype(jnp.bfloat16)
    table_imag = (-joined[None] * jnp.sin(psi)).astype(jnp.bfloat16)
    return (table_real, table_imag)


def pack_slots(owners, dest_count, capacity, members):
    matches = (owners[:, None] == jnp.arange(dest_count)[None, :]).astype(jnp.int32)
    ranking = jnp.sum((jnp.cumsum(matches, axis=0) - matches) * matches, axis=1)
    slot_index = owners * capacity + ranking
    source_row = (
        jnp.full((dest_count * capacity,), owners.shape[0], jnp.int32)
        .at[slot_index]
        .set(jnp.arange(owners.shape[0], dtype=jnp.int32))
    )
    padded = [
        jnp.concatenate([member, jnp.zeros((1,) + member.shape[1:], member.dtype)])
        for member in members
    ]
    return tuple((array_now[source_row] for array_now in padded))


def interior_part(x_edges, send_list, connectivity, elem_mats, elem_live):
    owned_rows, columns = x_edges.shape
    partitions, slot_width = send_list.shape
    element_count = connectivity.shape[1]
    padded = jnp.concatenate([x_edges, jnp.zeros((1, columns), x_edges.dtype)])
    outgoing = padded[send_list]
    received = lax.all_to_all(outgoing, ("dom", "dir"), split_axis=0, concat_axis=0, tiled=True)
    edge_table = jnp.concatenate([x_edges, received.reshape(partitions * slot_width, columns)])
    gathered = edge_table[connectivity]
    live_mask = (jnp.arange(element_count) < elem_live[0])[:, None]
    term_list = []
    for row_index in range(6):
        summed = jnp.zeros((element_count, columns), jnp.float32)
        for col_index in range(6):
            summed = summed + elem_mats[row_index * 6 + col_index][:, None] * gathered[col_index]
        term_list.append(jnp.where(live_mask, summed, jnp.zeros_like(summed)))
    stacked = jnp.stack(term_list).reshape(6 * element_count, columns)
    assembled = jax.ops.segment_sum(
        stacked, connectivity.reshape(-1), num_segments=owned_rows + partitions * slot_width
    )
    back_terms = assembled[owned_rows:]
    returned = lax.all_to_all(
        back_terms.reshape(partitions, slot_width, columns),
        ("dom", "dir"),
        split_axis=0,
        concat_axis=0,
        tiled=True,
    )
    folded = jax.ops.segment_sum(
        returned.reshape(-1, columns), send_list.reshape(-1), num_segments=owned_rows + 1
    )
    return assembled[:owned_rows] + folded[:owned_rows]


def block_sums(leaf_ids, factors, blocks, cone_count):
    block_count, block_size, columns = blocks.shape
    rows = factors.shape[1]
    plane = NODES * NODES
    height = 2 * cone_count * NODES**3
    group = next(size for size in (8, 4, 2, 1) if block_count % size == 0)

    def kernel(leaf_ref, factor_ref, block_ref, out_ref):
        step = pl.program_id(0)

        @pl.when(step == 0)
        def _():
            out_ref[...] = jnp.zeros_like(out_ref)

        for g in range(group):
            pairs = factor_ref[g, :plane, :]
            first = factor_ref[g, plane : plane + NODES, :]
            pieces = []
            for wave in range(2 * cone_count):
                at = plane + NODES + wave
                scaled = first * factor_ref[g, at : at + 1, :]
                for digit in range(NODES):
                    pieces.append((scaled[digit : digit + 1] * pairs).astype(jnp.bfloat16))
            weights = jnp.concatenate(pieces, axis=0)
            product = jnp.dot(weights, block_ref[g], preferred_element_type=jnp.float32)
            leaf = leaf_ref[step * group + g]
            out_ref[leaf] += product

    return pl.pallas_call(
        kernel,
        out_shape=jax.ShapeDtypeStruct((LEAVES_DEV, height, columns), jnp.float32),
        grid_spec=pltpu.PrefetchScalarGridSpec(
            num_scalar_prefetch=1,
            grid=(block_count // group,),
            in_specs=[
                pl.BlockSpec((group, rows, block_size), lambda i, leaf: (i, 0, 0)),
                pl.BlockSpec((group, block_size, columns), lambda i, leaf: (i, 0, 0)),
            ],
            out_specs=pl.BlockSpec((LEAVES_DEV, height, columns), lambda i, leaf: (0, 0, 0)),
        ),
        cost_estimate=pl.CostEstimate(
            flops=2 * block_count * height * block_size * columns,
            bytes_accessed=block_count * block_size * (rows * 4 + columns * 2),
            transcendentals=0,
        ),
    )(leaf_ids, factors, blocks)


def expand_leaves(arrived_blocks, arrived_meta, waves):
    columns = arrived_blocks.shape[2]
    cone_count = waves.shape[1]
    square = NODES**3
    leaf_ids = arrived_meta[:, 3, 0].astype(jnp.int32)
    coords = arrived_meta[:, :3].astype(jnp.float32)
    second = lagrange(coords[:, 1])
    third = lagrange(coords[:, 2])
    pairs = (second[:, :, None] * third[:, None, :]).reshape(
        coords.shape[0], NODES * NODES, coords.shape[2]
    )
    phase = wave_phase(waves, coords)
    factors = jnp.concatenate(
        [pairs, lagrange(coords[:, 0]), jnp.cos(phase), -jnp.sin(phase)], axis=1
    )
    sums = block_sums(leaf_ids, factors, arrived_blocks, cone_count).reshape(
        LEAVES_DEV, 2, cone_count, square, columns
    )
    real_sum, imag_sum = sums[:, 0], sums[:, 1]
    node_phase = wave_phase(waves, node_coords())
    cosine = jnp.cos(node_phase)[None, :, :, None]
    sine_part = jnp.sin(node_phase)[None, :, :, None]
    leaf_real = (cosine * real_sum - sine_part * imag_sum).astype(jnp.bfloat16)
    leaf_imag = (cosine * imag_sum + sine_part * real_sum).astype(jnp.bfloat16)
    table_real, table_imag = m2m_tables(waves)
    child_real = leaf_real.reshape(LEAVES_DEV // 8, 8, cone_count, square, columns)
    child_imag = leaf_imag.reshape(LEAVES_DEV // 8, 8, cone_count, square, columns)
    parent_real = jnp.einsum(
        "cops,xocsn->xcpn", table_real, child_real, preferred_element_type=jnp.float32
    ) - jnp.einsum("cops,xocsn->xcpn", table_imag, child_imag, preferred_element_type=jnp.float32)
    parent_imag = jnp.einsum(
        "cops,xocsn->xcpn", table_real, child_imag, preferred_element_type=jnp.float32
    ) + jnp.einsum("cops,xocsn->xcpn", table_imag, child_real, preferred_element_type=jnp.float32)
    return jnp.stack([parent_real, parent_imag], axis=2)


def boundary_part(currents, positions, block_live, block_owner, block_leaf, cone_waves):
    block_count, block_size, columns = currents.shape
    dom_count = lax.axis_size("dom")
    capacity = 3 * block_count // dom_count
    live_mask = jnp.arange(block_size)[None, :] < block_live[:, None]
    masked = jnp.where(live_mask[:, :, None], currents, jnp.zeros_like(currents))
    leaf_row = jnp.broadcast_to(
        block_leaf.astype(jnp.bfloat16)[:, None, None], (block_count, 1, block_size)
    )
    described = jnp.concatenate([positions, leaf_row], axis=1)
    packed_blocks, packed_meta = pack_slots(block_owner, dom_count, capacity, (masked, described))
    owner_blocks, owner_meta = (
        lax.all_to_all(packed_blocks, "dom", split_axis=0, concat_axis=0, tiled=True),
        lax.all_to_all(packed_meta, "dom", split_axis=0, concat_axis=0, tiled=True),
    )
    arrived_blocks, arrived_meta = (
        lax.all_gather(owner_blocks, "dir", axis=0, tiled=True),
        lax.all_gather(owner_meta, "dir", axis=0, tiled=True),
    )
    parents = expand_leaves(arrived_blocks, arrived_meta, cone_waves)
    return parents


def shards(
    x_edges,
    send_list,
    connectivity,
    elem_mats,
    elem_live,
    currents,
    positions,
    block_live,
    block_owner,
    block_leaf,
    cone_waves,
):
    interior_out = interior_part(x_edges, send_list, connectivity, elem_mats, elem_live)
    expansions = boundary_part(currents, positions, block_live, block_owner, block_leaf, cone_waves)
    return (interior_out, expansions)


def solution(mesh):
    placed = (
        P(("dom", "dir"), None),
        P(("dom", "dir"), None),
        P(None, ("dom", "dir")),
        P(None, ("dom", "dir")),
        P(("dom", "dir")),
        P(("dom", "dir"), None, None),
        P(("dom", "dir"), None, None),
        P(("dom", "dir")),
        P(("dom", "dir")),
        P(("dom", "dir")),
        P(None, "dir"),
    )
    return jax.shard_map(
        shards,
        mesh=mesh,
        in_specs=placed,
        out_specs=(P(("dom", "dir"), None), P("dom", "dir", None, None, None)),
        check_vma=False,
    )
```

profile of v0, /device:TPU:0, one launch (start us, length us, event | category | flops | bytes accessed | tf_op | source)
XLA Modules:
  0.0 344.2 jit_solution(2901099271363651961)
XLA Ops:
  13.6 2.7 gather_fusion.3
  16.3 78.1 %all_to_all.20 = bf16[96,128,128]{2,1,0:T(8,128)(2,1)} all-to-all(bf16[96,128,128]{2,1,0:T(8,128)(2,1)} %gather_fusion.3), channel_id=1, replica_groups=mesh['dom'=8,'dir'=4] {'dom'}, dimensions={0} | all-to-all | bytes 6291456 | tf_op jit(solution)/shard_map/all_to_all | solution.py:232
  96.6 3.6 %all-to-all-start.2 = ((bf16[96,4,128]{2,1,0:T(4,128)(2,1)}), bf16[96,4,128]{2,1,0:T(4,128)(2,1)S(1)}, u32[]{:S(2)}, u32[]{:S(2)}) async-start(bf16[96,4,128]{2,1,0:T(4,128)(2,1)} %gather_fusion.2), calls=%async_computation.2 | async-start | bytes 196608 | tf_op jit(solution)/shard_map/all_to_all | solution.py:233
  116.0 2.6 fusion.83
  122.6 2.9 copy.38
  126.2 4.3 %gather_fusion = bf16[1024,128]{1,0:T(8,128)(2,1)} fusion(bf16[2049,128]{1,0:T(8,128)(2,1)S(1)} %concatenate.30, s32[1024]{0:T(1024)S(1)} %get-tuple-element.92), kind=kCustom, calls=%fused_computation | custom fusion | bytes 528384 | tf_op jit(solution)/shard_map/gather | solution.py:107
  133.9 6.1 %all-to-all-start = ((bf16[32,32,128]{2,1,0:T(8,128)(2,1)}), bf16[32,32,128]{2,1,0:T(8,128)(2,1)S(1)}, u32[]{:S(2)}, u32[]{:S(2)}) async-start(bf16[32,32,128]{2,1,0:T(8,128)(2,1)} %bitcast.2), calls=%async_computation | async-start | bytes 524288 | tf_op jit(solution)/shard_map/all_to_all | solution.py:108
  140.0 11.4 %all_gather.6 = bf16[384,4,128]{2,1,0:T(4,128)(2,1)S(1)} all-gather(bf16[96,4,128]{2,1,0:T(4,128)(2,1)S(1)} %all-to-all-done.2), channel_id=1, replica_groups=mesh['dom'=8,'dir'=4] {'dir'}, dimensions={0}, use_global_device_ids=true | all-gather | bytes 491520 | tf_op jit(solution)/shard_map/all_gather | solution.py:237
  151.6 4.0 %fusion.63 = (f32[384,1,128]{2,1,0:T(1,128)}, f32[384,1,128]{2,1,0:T(1,128)}, f32[384,1,128]{2,1,0:T(1,128)}) fusion(f32[]{:T(128)S(6)} %sub.382, f32[]{:T(128)S(6)} %sub.381, f32[]{:T(128)S(6)} %sub.380, f32[]{:T(128)} %bitcast.63, f32[]{:T(128)} %bitcast.64, f32[]{:T(128)} %bitcast.62, f32[384,3,128]{2,1,0:T(4,128)S(1)} %slice_convert_fusion), kind=kLoop, calls=%fused_computation.161 | loop fusion | flops 1179648 | bytes 1179672 | tf_op jit(solution)/shard_map/div | solution.py:25
  156.2 4.9 %fusion.65 = (f32[384,1,128]{2,1,0:T(1,128)}, f32[384,1,128]{2,1,0:T(1,128)}, f32[384,1,128]{2,1,0:T(1,128)}, f32[384,1,128]{2,1,0:T(1,128)}, f32[384,1,128]{2,1,0:T(1,128)}, /*index=5*/f32[384,1,128]{2,1,0:T(1,128)}) fusion(f32[]{:T(128)S(6)} %sub.388, f32[]{:T(128)S(6)} %sub.387, f32[]{:T(128)S(6)} %sub.386, f32[]{:T(128)} %bitcast.63, f32[]{:T(128)} %bitcast.62, ...), kind=kLoop, calls=%fused_computation.163 | loop fusion | flops 2015232 | bytes 1966128 | tf_op jit(solution)/shard_map/div | solution.py:25
  161.2 4.1 %fusion.54 = (f32[384,1,128]{2,1,0:T(1,128)}, f32[384,1,128]{2,1,0:T(1,128)}, f32[384,1,128]{2,1,0:T(1,128)}, f32[384,1,128]{2,1,0:T(1,128)}, f32[384,1,128]{2,1,0:T(1,128)}, /*index=5*/f32[384,1,128]{2,1,0:T(1,128)}) fusion(f32[]{:T(128)S(6)} %sub.377, f32[]{:T(128)S(6)} %sub.374, f32[]{:T(128)S(6)} %sub.371, f32[]{:T(128)} %bitcast.63, f32[]{:T(128)} %bitcast.64, ...), kind=kLoop, calls=%fused_computation.152 | loop fusion | flops 1081344 | bytes 1966116 | tf_op jit(solution)/shard_map/div | solution.py:25
  165.4 18.1 %gather_fusion.1 = bf16[6144,128]{1,0:T(8,128)(2,1)S(1)} fusion(bf16[3072,128]{1,0:T(8,128)(2,1)S(1)} %pad_maximum_fusion, s32[6144]{0:T(1024)S(1)} %broadcast_clamp_fusion), kind=kCustom, calls=%fused_computation.1 | custom fusion | bytes 3170304 | tf_op jit(solution)/shard_map/gather | solution.py:110
  193.0 33.9 %scatter_custom_fusion = f32[3072,128]{1,0:T(8,128)S(1)} fusion(s32[6144]{0:T(1024)S(1)} %reshape.1008, f32[6144,128]{1,0:T(8,128)} %bitcast.228, f32[]{:T(128)} %constant.133.clone.1), kind=kCustom, calls=%fused_computation.65 | custom fusion | flops 786432 | bytes 1573376 | tf_op jit(solution)/shard_map/scatter-add | solution.py:119
  227.9 4.8 %all-to-all-start.1 = ((f32[32,32,128]{2,1,0:T(8,128)}), f32[32,32,128]{2,1,0:T(8,128)}, u32[]{:S(2)}, u32[]{:S(2)}) async-start(f32[32,32,128]{2,1,0:T(8,128)} %bitcast.52), calls=%async_computation.1 | async-start | bytes 1048576 | tf_op jit(solution)/shard_map/all_to_all | solution.py:123
  236.3 6.9 %sine_negate_fusion = (f32[384,4,128]{2,1,0:T(4,128)}, f32[384,4,128]{2,1,0:T(4,128)}) fusion(f32[384,128]{1,0:T(8,128)S(1)} %bitcast.227, f32[4]{0:T(128)S(1)} %copy-done.54, f32[384,128]{1,0:T(8,128)S(1)} %bitcast.226, f32[4]{0:T(128)S(1)} %copy-done.56, f32[384,128]{1,0:T(8,128)S(1)} %bitcast.225, f32[4]{0:T(128)S(1)} %copy-done.52), kind=kLoop, calls=%fused_computation.63 | loop fusion | flops 1179648 | bytes 2162736 | tf_op jit(solution)/shard_map/neg | solution.py:197
  244.0 14.5 %concatenate.34.factor_ref = f32[384,28,128]{2,1,0:T(8,128)} concatenate(f32[384,16,128]{2,1,0:T(8,128)S(1)} %bitcast.218, f32[384,1,128]{2,1,0:T(1,128)} %get-tuple-element.19, f32[384,1,128]{2,1,0:T(1,128)} %get-tuple-element.29, f32[384,1,128]{2,1,0:T(1,128)} %get-tuple-element.15, f32[384,1,128]{2,1,0:T(1,128)} %get-tuple-element.14, f32[384,4,128]{2,1,0:T(4,128)} %get-tuple-element.33, ...), dimensions={1} | concatenate | bytes 11010048 | tf_op jit(solution)/shard_map/concatenate | solution.py:196
  258.5 7.5 %fusion.53.leaf_ref = s32[384]{0:T(512)} fusion(bf16[384,4,128]{2,1,0:T(4,128)(2,1)S(1)} %all_gather.6), kind=kLoop, calls=%fused_computation.151 | loop fusion | flops 384 | bytes 2304 | tf_op jit(solution)/shard_map/convert_element_type | solution.py:188
  266.0 7.4 %scatter_custom_fusion.1 = f32[2049,128]{1,0:T(8,128)S(1)} fusion(s32[1024]{0:T(1024)} %reshape.1016, f32[1024,128]{1,0:T(8,128)} %bitcast.53, f32[]{:T(128)} %constant.133.clone.1), kind=kCustom, calls=%fused_computation.68 | custom fusion | flops 131072 | bytes 1049600 | tf_op jit(solution)/shard_map/scatter-add | solution.py:130
  275.6 40.2 %shard_map.122 = f32[16,512,128]{2,1,0:T(8,128)} custom-call(s32[384]{0:T(512)} %fusion.53.leaf_ref, f32[384,28,128]{2,1,0:T(8,128)} %concatenate.34.factor_ref, bf16[384,128,128]{2,1,0:T(8,128)(2,1)} %all-gather.2.cloned.1.call-done.block_ref), custom_call_target="tpu_custom_call" | custom-call | flops 6442450944 | bytes 18087936 | tf_op jit(solution)/shard_map/pallas_call | solution.py:164
  315.8 2.8 fusion.105
  320.7 3.9 %convolution_bitcast_fusion.2 = f32[4,2,128,64]{2,3,1,0:T(8,128)S(1)} fusion(bf16[2,8,4,64,128]{4,3,1,0,2:T(8,128)(2,1)S(1)} %get-tuple-element.10, f32[8,64,64]{2,1,0:T(8,128)S(1)} %copy-done.11, f32[8,64,64]{2,1,0:T(8,128)S(1)} %copy-done.13, f32[4]{0:T(128)S(1)} %copy-done.54, f32[8,64,64]{2,1,0:T(8,128)S(1)} %copy-done.14, f32[4]{0:T(128)S(1)} %copy-done.56, ...), kind=kOutput, calls=%fused_computation.48 | convolution fusion | flops 68157440 | bytes 1835056 | tf_op jit(solution)/shard_map/cops,xocsn->xcpn/dot_general | solution.py:213
  324.6 3.9 %convolution_bitcast_fusion = f32[4,2,128,64]{2,3,1,0:T(8,128)S(1)} fusion(bf16[2,8,4,64,128]{4,3,1,0,2:T(8,128)(2,1)S(1)} %get-tuple-element.11, f32[8,64,64]{2,1,0:T(8,128)S(1)} %copy-done.11, f32[8,64,64]{2,1,0:T(8,128)S(1)} %copy-done.13, f32[4]{0:T(128)S(1)} %copy-done.54, f32[8,64,64]{2,1,0:T(8,128)S(1)} %copy-done.14, f32[4]{0:T(128)S(1)} %copy-done.56, ...), kind=kOutput, calls=%fused_computation.46 | convolution fusion | flops 68157440 | bytes 1835056 | tf_op jit(solution)/shard_map/cops,xocsn->xcpn/dot_general | solution.py:216
  328.4 4.0 %fusion.1 = f32[2,4,1,64,128]{4,3,0,1,2:T(8,128)S(1)} fusion(f32[4,2,128,64]{2,3,1,0:T(8,128)S(1)} %convolution_bitcast_fusion.2, bf16[2,8,4,64,128]{4,3,1,0,2:T(8,128)(2,1)S(1)} %get-tuple-element.11, f32[8,64,64]{2,1,0:T(8,128)S(1)} %copy-done.13, f32[4]{0:T(128)S(1)} %copy-done.54, f32[8,64,64]{2,1,0:T(8,128)S(1)} %copy-done.14, f32[4]{0:T(128)S(1)} %copy-done.56, ...), kind=kOutput, calls=%fused_computation.51 | convolution fusion | flops 68222976 | bytes 2097200 | tf_op jit(solution)/shard_map/cops,xocsn->xcpn/dot_general | solution.py:211
  332.4 3.8 %fusion.3 = f32[2,4,1,64,128]{4,3,0,1,2:T(8,128)S(1)} fusion(f32[4,2,128,64]{2,3,1,0:T(8,128)S(1)} %convolution_bitcast_fusion, bf16[2,8,4,64,128]{4,3,1,0,2:T(8,128)(2,1)S(1)} %get-tuple-element.10, f32[8,64,64]{2,1,0:T(8,128)S(1)} %copy-done.13, f32[4]{0:T(128)S(1)} %copy-done.54, f32[8,64,64]{2,1,0:T(8,128)S(1)} %copy-done.14, f32[4]{0:T(128)S(1)} %copy-done.56, ...), kind=kOutput, calls=%fused_computation.53 | convolution fusion | flops 68222976 | bytes 2097200 | tf_op jit(solution)/shard_map/cops,xocsn->xcpn/dot_general | solution.py:214
  (191 shorter events, 37.1 us)
Async XLA Ops:
  7.2 268.5 %all-gather.2.cloned.1.call-start = ((), (), s32[]{:S(2)}) async-start(), calls=%async_computation.4 | async-start | bytes 15728640 | tf_op jit(solution)/shard_map/all_gather | solution.py:236
  96.6 37.3 %all-to-all-start.2 = ((bf16[96,4,128]{2,1,0:T(4,128)(2,1)}), bf16[96,4,128]{2,1,0:T(4,128)(2,1)S(1)}, u32[]{:S(2)}, u32[]{:S(2)}) async-start(bf16[96,4,128]{2,1,0:T(4,128)(2,1)} %gather_fusion.2), calls=%async_computation.2 | async-start | bytes 196608 | tf_op jit(solution)/shard_map/all_to_all | solution.py:233
  130.7 20.9 %copy-start.51 = (f32[4]{0:T(128)}, f32[4]{0:T(128)S(1)}, u32[]{:S(2)}) copy-start(f32[4]{0:T(128)S(1)} %get-tuple-element.82) | copy-start | bytes 52
  130.7 20.9 %copy-start.53 = (f32[4]{0:T(128)}, f32[4]{0:T(128)S(1)}, u32[]{:S(2)}) copy-start(f32[4]{0:T(128)S(1)} %get-tuple-element.83) | copy-start | bytes 52
  130.7 20.9 %copy-start.55 = (f32[4]{0:T(128)}, f32[4]{0:T(128)S(1)}, u32[]{:S(2)}) copy-start(f32[4]{0:T(128)S(1)} %get-tuple-element.84) | copy-start | bytes 52
  133.9 31.4 %all-to-all-start = ((bf16[32,32,128]{2,1,0:T(8,128)(2,1)}), bf16[32,32,128]{2,1,0:T(8,128)(2,1)S(1)}, u32[]{:S(2)}, u32[]{:S(2)}) async-start(bf16[32,32,128]{2,1,0:T(8,128)(2,1)} %bitcast.2), calls=%async_computation | async-start | bytes 524288 | tf_op jit(solution)/shard_map/all_to_all | solution.py:108
  165.4 18.2 %copy-start.40 = (f32[1,1024]{1,0:T(1,128)S(1)}, f32[1,1024]{1,0:T(1,128)}, u32[]{:S(2)}) copy-start(f32[1,1024]{1,0:T(1,128)} %get-tuple-element.63) | copy-start | bytes 12292
  165.4 18.2 %copy-start.41 = (f32[1,1024]{1,0:T(1,128)S(1)}, f32[1,1024]{1,0:T(1,128)}, u32[]{:S(2)}) copy-start(f32[1,1024]{1,0:T(1,128)} %get-tuple-element.64) | copy-start | bytes 12292
  165.4 18.2 %copy-start.42 = (f32[1,1024]{1,0:T(1,128)S(1)}, f32[1,1024]{1,0:T(1,128)}, u32[]{:S(2)}) copy-start(f32[1,1024]{1,0:T(1,128)} %get-tuple-element.65) | copy-start | bytes 12292
  165.4 18.2 %copy-start.43 = (f32[1,1024]{1,0:T(1,128)S(1)}, f32[1,1024]{1,0:T(1,128)}, u32[]{:S(2)}) copy-start(f32[1,1024]{1,0:T(1,128)} %get-tuple-element.66) | copy-start | bytes 12292
  165.4 18.2 %copy-start.44 = (f32[1,1024]{1,0:T(1,128)S(1)}, f32[1,1024]{1,0:T(1,128)}, u32[]{:S(2)}) copy-start(f32[1,1024]{1,0:T(1,128)} %get-tuple-element.67) | copy-start | bytes 12292
  165.4 18.2 %copy-start.45 = (f32[1,1024]{1,0:T(1,128)S(1)}, f32[1,1024]{1,0:T(1,128)}, u32[]{:S(2)}) copy-start(f32[1,1024]{1,0:T(1,128)} %get-tuple-element.68) | copy-start | bytes 12292
  193.0 39.7 %copy-start.3 = (f32[384,1,128]{2,1,0:T(1,128)S(1)}, f32[384,1,128]{2,1,0:T(1,128)}, u32[]{:S(2)}) copy-start(f32[384,1,128]{2,1,0:T(1,128)} %get-tuple-element.16) | copy-start | bytes 589828
  193.0 39.7 %copy-start.4 = (f32[384,1,128]{2,1,0:T(1,128)S(1)}, f32[384,1,128]{2,1,0:T(1,128)}, u32[]{:S(2)}) copy-start(f32[384,1,128]{2,1,0:T(1,128)} %get-tuple-element.18) | copy-start | bytes 589828
  227.0 9.2 %copy-start = (f32[3072,128]{1,0:T(8,128)}, f32[3072,128]{1,0:T(8,128)S(1)}, u32[]{:S(2)}) copy-start(f32[3072,128]{1,0:T(8,128)S(1)} %scatter_custom_fusion) | copy-start | bytes 4718596
  227.0 7.5 %copy-start.2 = (f32[384,1,128]{2,1,0:T(1,128)S(1)}, f32[384,1,128]{2,1,0:T(1,128)}, u32[]{:S(2)}) copy-start(f32[384,1,128]{2,1,0:T(1,128)} %get-tuple-element.17) | copy-start | bytes 589828
  227.0 7.5 %copy-start.8 = (f32[384,1,128]{2,1,0:T(1,128)S(1)}, f32[384,1,128]{2,1,0:T(1,128)}, u32[]{:S(2)}) copy-start(f32[384,1,128]{2,1,0:T(1,128)} %get-tuple-element.20) | copy-start | bytes 589828
  227.8 8.4 %copy-start.5 = (f32[384,1,128]{2,1,0:T(1,128)S(1)}, f32[384,1,128]{2,1,0:T(1,128)}, u32[]{:S(2)}) copy-start(f32[384,1,128]{2,1,0:T(1,128)} %get-tuple-element.26) | copy-start | bytes 589828
  227.8 8.4 %copy-start.6 = (f32[384,1,128]{2,1,0:T(1,128)S(1)}, f32[384,1,128]{2,1,0:T(1,128)}, u32[]{:S(2)}) copy-start(f32[384,1,128]{2,1,0:T(1,128)} %get-tuple-element.27) | copy-start | bytes 589828
  227.8 8.4 %copy-start.7 = (f32[384,1,128]{2,1,0:T(1,128)S(1)}, f32[384,1,128]{2,1,0:T(1,128)}, u32[]{:S(2)}) copy-start(f32[384,1,128]{2,1,0:T(1,128)} %get-tuple-element.28) | copy-start | bytes 589828
  227.8 8.4 %copy-start.52 = (f32[4]{0:T(128)S(1)}, f32[4]{0:T(128)}, u32[]{:S(2)}) copy-start(f32[4]{0:T(128)} %copy-done.51) | copy-start | bytes 52
  227.8 8.4 %copy-start.54 = (f32[4]{0:T(128)S(1)}, f32[4]{0:T(128)}, u32[]{:S(2)}) copy-start(f32[4]{0:T(128)} %copy-done.53) | copy-start | bytes 52
  227.8 8.4 %copy-start.56 = (f32[4]{0:T(128)S(1)}, f32[4]{0:T(128)}, u32[]{:S(2)}) copy-start(f32[4]{0:T(128)} %copy-done.55) | copy-start | bytes 52
  227.9 38.1 %all-to-all-start.1 = ((f32[32,32,128]{2,1,0:T(8,128)}), f32[32,32,128]{2,1,0:T(8,128)}, u32[]{:S(2)}, u32[]{:S(2)}) async-start(f32[32,32,128]{2,1,0:T(8,128)} %bitcast.52), calls=%async_computation.1 | async-start | bytes 1048576 | tf_op jit(solution)/shard_map/all_to_all | solution.py:123
  (39 other events, 93.1 us)
Sparse Core Ops, SparseCore 0:
  94.5 86.0 all-gather.1
where the time goes:
time: 350 us; the launch traced here: 344 us
  other arithmetic  94.7 us (27%)
  blocking collectives  89.5 us (26%)
  local copies, waits for them, and re-layouts  58.7 us (17%)
  Pallas kernels  40.2 us (11%)
  between operations  30.9 us (9%)
  matrix products  15.5 us (4%)
  starting transfers between devices  14.6 us (4%)
    all_to_all x1, blocking collectives, boundary_part(): lax.all_to_all(packed_blocks, 'dom', split_axis=0, concat_axis=0, tiled=T...  78.1 us
    pallas_call x1, Pallas kernels, block_sums(): pl.pallas_call(kernel, out_shape=jax.ShapeDtypeStruct((LEAVES_DEV, height...  40.2 us
    scatter-add x1, other arithmetic, interior_part(): jax.ops.segment_sum(stacked, connectivity.reshape(-1), num_segments=owned...  33.9 us
    gather x1, local copies, waits for them, and re-layouts, interior_part(): gathered = edge_table[connectivity]  18.1 us
    div x4, other arithmetic, lagrange(): product * (points - node_values[other_node])  15.6 us
    concatenate x1, local copies, waits for them, and re-layouts, expand_leaves(): jnp.concatenate([pairs, lagrange(coords[:, 0]), jnp.cos(phase), -jnp.sin(...  14.5 us
    all_gather x1, blocking collectives, boundary_part(): lax.all_gather(owner_meta, 'dir', axis=0, tiled=True)  11.4 us
    convert_element_type x1, other arithmetic, expand_leaves(): leaf_ids = arrived_meta[:, 3, 0].astype(jnp.int32)  7.48 us
  transfers between devices with their start and end apart: 4, of which 0 were waited for; matrix products, arithmetic and copies ran while one was open for 40% of the time, Pallas kernels for 0%

commit v1 on v0

v1 whole, which is shorter than its diff:
```python
import math

import jax
import jax.numpy as jnp
from jax import lax
from jax.experimental import pallas as pl
from jax.experimental.pallas import tpu as pltpu
from jax.sharding import PartitionSpec as P

LEAVES_DEV = 16
OCTANTS = 8
NODES = 4
PLANE = NODES * NODES
SQUARE = NODES**3
POINTS = [math.cos((2 * j + 1) * math.pi / (2 * NODES)) for j in range(NODES)]
META = 6


def lagrange_rows(v):
    rows = []
    for target in range(NODES):
        product = None
        scale = 1.0
        for other in range(NODES):
            if other != target:
                factor = v - POINTS[other]
                product = factor if product is None else product * factor
                scale *= POINTS[target] - POINTS[other]
        rows.append(product * (1.0 / scale))
    return rows


def cos_sin(phase):
    turns = jnp.floor(phase * (1.0 / math.pi) + 0.5)
    odd = turns - 2.0 * jnp.floor(turns * 0.5)
    sign = 1.0 - 2.0 * odd
    high = 3.140625
    rest = (phase - turns * high) - turns * (math.pi - high)
    square = rest * rest
    cosine = jnp.full_like(rest, 1.0 / math.factorial(12))
    for order in (10, 8, 6, 4, 2, 0):
        cosine = cosine * square + (1.0 if order % 4 == 0 else -1.0) / math.factorial(order)
    sine = jnp.full_like(rest, -1.0 / math.factorial(11))
    for order in (9, 7, 5, 3, 1):
        sine = sine * square + (1.0 if order % 4 == 1 else -1.0) / math.factorial(order)
    return cosine * sign, sine * rest * sign


def xor_pairs(count, bit):
    return [(i, i ^ (1 << bit)) for i in range(count)]


def log2(count):
    bits = count.bit_length() - 1
    if count != 1 << bits:
        raise ValueError("axis size")
    return bits


def spread(value, axis, bits):
    held = [value]
    count = lax.axis_size(axis)
    for bit in bits:
        held = held + [lax.ppermute(h, axis, xor_pairs(count, bit)) for h in held]
    return held


def block_sums(slots, waves, metas, blocks, previous, slot_count, cone_count, chunks):
    lists = len(metas)
    per_list, block_size, columns = blocks[0].shape
    height = 2 * cone_count * SQUARE
    firsts = 2 * cone_count * NODES
    rows = PLANE + firsts
    group = 16
    half = slot_count // 2
    piece = height // chunks if chunks else height

    def kernel(*refs):
        slot_ref, wave_ref = refs[:2]
        meta_refs = refs[2 : 2 + lists]
        block_refs = refs[2 + lists : 2 + 2 * lists]
        at = 2 + 2 * lists
        if previous is not None:
            before_ref = refs[at]
            at += 1
        outs = refs[at:-2] if chunks else refs[at:-1]
        factor_ref = refs[-1]
        sum_ref = refs[-2] if chunks else outs[0]

        for which in range(lists):
            for part in range(per_list // group):
                span = pl.ds(part * group, group)
                meta = [meta_refs[which][row, span, :].astype(jnp.float32) for row in range(META)]
                octant = meta[3] - 8.0 * jnp.floor(meta[3] * 0.125)
                high = jnp.floor(octant * 0.25)
                middle = jnp.floor((octant - 4.0 * high) * 0.5)
                low = octant - 4.0 * high - 2.0 * middle
                double = [2.0 * bit - 1.0 + pos for bit, pos in zip((high, middle, low), meta[:3])]
                lanes = lax.broadcasted_iota(jnp.int32, (group, block_size), 1).astype(jnp.float32)
                live = lanes < meta[4]
                first = [jnp.where(live, r, 0.0) for r in lagrange_rows(0.5 * double[0])]
                second = lagrange_rows(0.5 * double[1])
                third = lagrange_rows(0.5 * double[2])
                start = (which * per_list + part * group) * rows

                def put(row, value):
                    factor_ref[pl.ds(start + row, group, stride=rows), :] = value

                for a in range(NODES):
                    for b in range(NODES):
                        put(a * NODES + b, second[a] * third[b])
                for cone in range(cone_count):
                    phase = (
                        wave_ref[0, cone] * double[0]
                        + wave_ref[1, cone] * double[1]
                        + wave_ref[2, cone] * double[2]
                    )
                    cosine, sine = cos_sin(phase)
                    for digit in range(NODES):
                        put(PLANE + cone * 2 * NODES + digit, first[digit] * cosine)
                        put(PLANE + cone * 2 * NODES + NODES + digit, first[digit] * -sine)

        sum_ref[...] = jnp.zeros_like(sum_ref)
        for which in range(lists):

            def one(index, carry):
                base = pl.multiple_of((which * per_list + index) * rows, 8)
                pairs = factor_ref[pl.ds(base, PLANE), :]
                pieces = [
                    (factor_ref[pl.ds(base + PLANE + row, 1), :] * pairs).astype(jnp.bfloat16)
                    for row in range(firsts)
                ]
                weights = jnp.concatenate(pieces, axis=0)
                product = jnp.dot(
                    weights, block_refs[which][index], preferred_element_type=jnp.float32
                )
                slot = slot_ref[which * per_list + index]
                sum_ref[slot] += product
                return carry

            lax.fori_loop(0, per_list, one, 0, unroll=2)

        if chunks:

            def finish(slot, carry):
                for chunk in range(chunks):
                    span = pl.ds(chunk * piece, piece)
                    keep = sum_ref[slot, span, :]
                    send = sum_ref[half + slot, span, :]
                    if previous is not None:
                        keep += before_ref[slot, span, :]
                        send += before_ref[half + slot, span, :]
                    outs[chunk][slot] = keep
                    outs[chunks + chunk][slot] = send.astype(jnp.bfloat16)
                return carry

            lax.fori_loop(0, half, finish, 0)

    whole = jax.ShapeDtypeStruct((slot_count, height, columns), jnp.float32)
    if chunks:
        out_shape = [jax.ShapeDtypeStruct((half, piece, columns), jnp.float32)] * chunks + [
            jax.ShapeDtypeStruct((half, piece, columns), jnp.bfloat16)
        ] * chunks
    else:
        out_shape = [whole]
    vmem = pl.BlockSpec(memory_space=pltpu.VMEM)
    smem = pl.BlockSpec(memory_space=pltpu.SMEM)
    scratch = [pltpu.VMEM((lists * per_list * rows, block_size), jnp.float32)]
    if chunks:
        scratch = [pltpu.VMEM(whole.shape, jnp.float32)] + scratch
    operands = [slots, waves, *metas, *blocks] + ([previous] if previous is not None else [])
    total = lists * per_list
    return pl.pallas_call(
        kernel,
        out_shape=out_shape,
        in_specs=[smem, smem] + [vmem] * (len(operands) - 2),
        out_specs=[vmem] * len(out_shape),
        scratch_shapes=scratch,
        compiler_params=pltpu.CompilerParams(vmem_limit_bytes=48 << 20),
        cost_estimate=pl.CostEstimate(
            flops=2 * total * height * block_size * columns,
            bytes_accessed=total * block_size * columns * 2 + slot_count * height * columns * 4,
            transcendentals=0,
        ),
    )(*operands)


def boundary_part(currents, positions, block_live, block_owner, block_leaf, cone_waves):
    block_count, block_size, columns = currents.shape
    cone_count = cone_waves.shape[1]
    dom_count, dir_count = lax.axis_size("dom"), lax.axis_size("dir")
    parents = LEAVES_DEV // OCTANTS
    slot_count = dom_count * parents
    dom_bits, dir_bits = log2(dom_count), log2(dir_count)

    numbers = jnp.stack([block_leaf, block_live, block_owner]).astype(jnp.bfloat16)
    meta = jnp.concatenate(
        [
            positions.transpose(1, 0, 2),
            jnp.broadcast_to(numbers[:, :, None], (3, block_count, block_size)),
        ],
        axis=0,
    )
    low = list(range(dir_bits - 1))
    groups = []
    far = lax.ppermute(currents, "dir", xor_pairs(dir_count, dir_bits - 1))
    far_meta = lax.ppermute(meta, "dir", xor_pairs(dir_count, dir_bits - 1))
    groups.append((spread(meta, "dir", low), spread(currents, "dir", low)))
    groups.append((spread(far_meta, "dir", low), spread(far, "dir", low)))

    me = lax.axis_index("dom")

    def slots_of(metas):
        ints = jnp.stack([m[3:META, :, 0] for m in metas], axis=1).astype(jnp.int32)
        leaf, owner = ints[0].reshape(-1), ints[2].reshape(-1)
        relative = owner ^ me
        order = jnp.zeros_like(relative)
        for bit in range(dom_bits):
            order = order | (((relative >> bit) & 1) << (dom_bits - 1 - bit))
        return order * parents + leaf // OCTANTS

    chunks = cone_count
    (near,) = block_sums(
        slots_of(groups[0][0]), cone_waves, *groups[0], None, slot_count, cone_count, 0
    )
    pieces = block_sums(
        slots_of(groups[1][0]), cone_waves, *groups[1], near, slot_count, cone_count, chunks
    )
    keeps, sends = list(pieces[:chunks]), list(pieces[chunks:])
    size = slot_count // 2
    for bit in range(dom_bits):
        next_keeps, next_sends = [], []
        for keep, send in zip(keeps, sends):
            got = lax.ppermute(send, "dom", xor_pairs(dom_count, bit))
            if bit < dom_bits - 1:
                lower = size // 2
                next_keeps.append(keep[:lower] + got[:lower].astype(jnp.float32))
                next_sends.append(
                    (keep[lower:] + got[lower:].astype(jnp.float32)).astype(jnp.bfloat16)
                )
            else:
                next_keeps.append(keep + got.astype(jnp.float32))
        keeps, sends = next_keeps, next_sends
        size //= 2
    digits = jnp.arange(SQUARE)
    digits = jnp.stack([digits // PLANE, digits // NODES % NODES, digits % NODES])
    nodes = jnp.cos((2.0 * digits.astype(jnp.float32) + 1.0) * (math.pi / (2.0 * NODES)))
    angle = 2.0 * (
        cone_waves[0][:, None] * nodes[0]
        + cone_waves[1][:, None] * nodes[1]
        + cone_waves[2][:, None] * nodes[2]
    )
    cosine, sine = jnp.cos(angle), jnp.sin(angle)
    outs = []
    per = cone_count // chunks
    for chunk, keep in enumerate(keeps):
        parts = keep.reshape(parents, per, 2, SQUARE, columns)
        c = cosine[chunk * per : (chunk + 1) * per][None, :, :, None]
        s = sine[chunk * per : (chunk + 1) * per][None, :, :, None]
        real, imag = parts[:, :, 0], parts[:, :, 1]
        outs.append(jnp.stack([c * real - s * imag, c * imag + s * real], axis=2))
    return jnp.concatenate(outs, axis=1)


def element_sums(links, live, x_edges, received, mats, owned_rows):
    edges, element_count = links.shape
    columns = x_edges.shape[1]
    halo = received.shape[0]
    table_rows = owned_rows + halo
    step = 8

    def kernel(link_ref, live_ref, x_ref, halo_ref, mat_ref, own_ref, back_ref, *scratch):
        table_ref, got_ref, term_ref = scratch[:3]
        sums = scratch[3:]
        table_ref[pl.ds(0, owned_rows), :] = x_ref[...].astype(jnp.float32)
        table_ref[pl.ds(owned_rows, halo), :] = halo_ref[...].astype(jnp.float32)
        for ref in sums:
            ref[...] = jnp.zeros_like(ref)

        def one(index, carry):
            start = pl.multiple_of(index * step, step)
            for edge in range(edges):
                for lane in range(step):
                    row = link_ref[edge, start + lane]
                    got_ref[edge, pl.ds(lane, 1), :] = table_ref[pl.ds(row, 1), :]
            number = start + lax.broadcasted_iota(jnp.int32, (step, mat_ref.shape[1]), 0)
            mat = jnp.where(number < live_ref[0], mat_ref[pl.ds(start, step), :], 0.0)
            got = [got_ref[edge] for edge in range(edges)]
            for i in range(edges):
                total = None
                for j in range(edges):
                    at = edges * i + j
                    term = mat[:, at : at + 1] * got[j]
                    total = term if total is None else total + term
                term_ref[i] = total
            for lane in range(step):
                for edge in range(edges):
                    row = link_ref[edge, start + lane]
                    sums[edge][pl.ds(row, 1), :] += term_ref[edge, pl.ds(lane, 1), :]
            return carry

        lax.fori_loop(0, element_count // step, one, 0)

        def total_of(span):
            total = sums[0][span, :]
            for ref in sums[1:]:
                total = total + ref[span, :]
            return total

        own_ref[...] = total_of(pl.ds(0, owned_rows))
        back_ref[...] = total_of(pl.ds(owned_rows, halo)).astype(jnp.bfloat16)

    vmem = pl.BlockSpec(memory_space=pltpu.VMEM)
    smem = pl.BlockSpec(memory_space=pltpu.SMEM)
    return pl.pallas_call(
        kernel,
        out_shape=[
            jax.ShapeDtypeStruct((owned_rows, columns), jnp.float32),
            jax.ShapeDtypeStruct((halo, columns), jnp.bfloat16),
        ],
        in_specs=[smem, smem, vmem, vmem, vmem],
        out_specs=[vmem, vmem],
        scratch_shapes=[
            pltpu.VMEM((table_rows, columns), jnp.float32),
            pltpu.VMEM((edges, step, columns), jnp.float32),
            pltpu.VMEM((edges, step, columns), jnp.float32),
        ]
        + [pltpu.VMEM((table_rows, columns), jnp.float32)] * edges,
        compiler_params=pltpu.CompilerParams(vmem_limit_bytes=56 << 20),
        cost_estimate=pl.CostEstimate(
            flops=4_000_000_000, bytes_accessed=table_rows * columns * 8, transcendentals=0
        ),
    )(links, live, x_edges, received, mats)


def fold_sums(rows, returned, owned):
    count, columns = returned.shape
    owned_rows = owned.shape[0]
    ways = 4

    def kernel(row_ref, back_ref, own_ref, out_ref, wide_ref, *sums):
        wide_ref[...] = back_ref[...].astype(jnp.float32)
        for ref in sums:
            ref[...] = jnp.zeros_like(ref)

        def one(index, carry):
            start = pl.multiple_of(index * 16, 16)
            for lane in range(16):
                row = row_ref[start + lane]
                sums[lane % ways][pl.ds(row, 1), :] += wide_ref[pl.ds(start + lane, 1), :]
            return carry

        lax.fori_loop(0, count // 16, one, 0)
        total = own_ref[...]
        for ref in sums:
            total = total + ref[...]
        out_ref[...] = total

    vmem = pl.BlockSpec(memory_space=pltpu.VMEM)
    return pl.pallas_call(
        kernel,
        out_shape=jax.ShapeDtypeStruct((owned_rows, columns), jnp.float32),
        in_specs=[pl.BlockSpec(memory_space=pltpu.SMEM), vmem, vmem],
        out_specs=vmem,
        scratch_shapes=[pltpu.VMEM((count, columns), jnp.float32)]
        + [pltpu.VMEM((owned_rows, columns), jnp.float32)] * ways,
        cost_estimate=pl.CostEstimate(
            flops=1_000_000_000, bytes_accessed=owned_rows * columns * 8, transcendentals=0
        ),
    )(rows, returned, owned)


def interior_part(x_edges, send_list, connectivity, elem_mats, elem_live):
    owned_rows, columns = x_edges.shape
    partitions, slot_width = send_list.shape
    rows = jnp.minimum(send_list, owned_rows - 1)
    outgoing = x_edges[rows]
    received = lax.all_to_all(outgoing, ("dom", "dir"), split_axis=0, concat_axis=0, tiled=True)
    owned, back = element_sums(
        connectivity,
        elem_live,
        x_edges,
        received.reshape(partitions * slot_width, columns),
        elem_mats.T,
        owned_rows,
    )
    returned = lax.all_to_all(
        back.reshape(partitions, slot_width, columns),
        ("dom", "dir"),
        split_axis=0,
        concat_axis=0,
        tiled=True,
    )
    return fold_sums(rows.reshape(-1), returned.reshape(partitions * slot_width, columns), owned)


def shards(
    x_edges,
    send_list,
    connectivity,
    elem_mats,
    elem_live,
    currents,
    positions,
    block_live,
    block_owner,
    block_leaf,
    cone_waves,
):
    interior_out = interior_part(x_edges, send_list, connectivity, elem_mats, elem_live)
    expansions = boundary_part(currents, positions, block_live, block_owner, block_leaf, cone_waves)
    return (interior_out, expansions)


def solution(mesh):
    placed = (
        P(("dom", "dir"), None),
        P(("dom", "dir"), None),
        P(None, ("dom", "dir")),
        P(None, ("dom", "dir")),
        P(("dom", "dir")),
        P(("dom", "dir"), None, None),
        P(("dom", "dir"), None, None),
        P(("dom", "dir")),
        P(("dom", "dir")),
        P(("dom", "dir")),
        P(None, "dir"),
    )
    return jax.shard_map(
        shards,
        mesh=mesh,
        in_specs=placed,
        out_specs=(P(("dom", "dir"), None), P("dom", "dir", None, None, None)),
        check_vma=False,
    )
```

time: 350 us -> 136 us (0.39); the launches traced: 344 us -> 135 us
  other arithmetic: 94.7 us -> 4.68 us
  blocking collectives: 89.5 us -> 0 us
  local copies, waits for them, and re-layouts: 58.7 us -> 11.5 us
  between operations: 30.9 us -> 1.5 us
  waiting for transfers between devices: 0.03 us -> 29.2 us
  starting transfers between devices: 14.6 us -> 33.5 us
  matrix products: 15.5 us -> 0 us
  Pallas kernels: 40.2 us -> 54.8 us
    all_to_all x1 -> x0, blocking collectives: 78.1 us -> none  [boundary_part(): lax.all_to_all(packed_blocks, 'dom', split_axis=0, concat_axis=0, tiled=T...]
    scatter-add x2 -> x0, other arithmetic: 41.3 us -> none  [the longest x1 33.9 us: interior_part(): jax.ops.segment_sum(stacked, connectivity.reshape(-1), num_segments=owned...]
    ppermute x0 -> x18, waiting for transfers between devices: none -> 29.2 us  [the longest x12 18.2 us: boundary_part(): got = lax.ppermute(send, 'dom', xor_pairs(dom_count, bit))]
    ppermute x0 -> x18, starting transfers between devices: none -> 22.1 us  [the longest x12 18.3 us: boundary_part(): got = lax.ppermute(send, 'dom', xor_pairs(dom_count, bit))]
    gather x4 -> x1, local copies, waits for them, and re-layouts: 26.4 us -> 5.19 us  [interior_part(): outgoing = x_edges[rows]]
    div x4 -> x0, other arithmetic: 15.6 us -> none  [lagrange(): product * (points - node_values[other_node])]
    dot_general x4 -> x0, matrix products: 15.5 us -> none  [the longest x1 4.01 us: expand_leaves(): jnp.einsum('cops,xocsn->xcpn', table_real, child_real, preferred_element_...]
    pallas_call x1 -> x4, Pallas kernels: 40.2 us -> 54.8 us  [the longest x1 27.1 us: element_sums(): pl.pallas_call(kernel, out_shape=[jax.ShapeDtypeStruct((owned_rows, colum...]
  transfers between devices with their start and end apart: 4 -> 20, of which waited for: 0 -> 9; matrix products, arithmetic and copies ran while one was open for 40% -> 8% of each run, Pallas kernels for 0% -> 41%
where the time goes in v1:
time: 136 us; the launch traced here: 135 us
  Pallas kernels  54.8 us (40%)
  starting transfers between devices  33.5 us (25%)
  waiting for transfers between devices  29.2 us (21%)
  local copies, waits for them, and re-layouts  11.5 us (8%)
  other arithmetic  4.68 us (3%)
  between operations  1.5 us (1%)
    pallas_call x1, Pallas kernels, element_sums(): pl.pallas_call(kernel, out_shape=[jax.ShapeDtypeStruct((owned_rows, colum...  27.1 us
    pallas_call x2, Pallas kernels, block_sums(): pl.pallas_call(kernel, out_shape=out_shape, in_specs=[smem, smem] + [vmem...  23.2 us
    ppermute x12, starting transfers between devices, boundary_part(): got = lax.ppermute(send, 'dom', xor_pairs(dom_count, bit))  18.3 us
    ppermute x12, waiting for transfers between devices, boundary_part(): got = lax.ppermute(send, 'dom', xor_pairs(dom_count, bit))  18.2 us
    ppermute x1, waiting for transfers between devices, boundary_part(): far = lax.ppermute(currents, 'dir', xor_pairs(dir_count, dir_bits - 1))  11 us
    all_to_all x1, starting transfers between devices, interior_part(): lax.all_to_all(outgoing, ('dom', 'dir'), split_axis=0, concat_axis=0, til...  6.07 us
    all_to_all x1, starting transfers between devices, interior_part(): lax.all_to_all(back.reshape(partitions, slot_width, columns), ('dom', 'di...  5.34 us
    gather x1, local copies, waits for them, and re-layouts, interior_part(): outgoing = x_edges[rows]  5.19 us
  transfers between devices with their start and end apart: 20, of which 9 were waited for; matrix products, arithmetic and copies ran while one was open for 8% of the time, Pallas kernels for 41%

profile of v1, /device:TPU:0, one launch (start us, length us, event | category | flops | bytes accessed | tf_op | source)
XLA Modules:
  0.0 135.1 jit_solution(17330198991015765619)
XLA Ops:
  3.3 2.6 %collective-permute-start = (bf16[6,32,128]{2,1,0:T(8,128)(2,1)S(1)}, bf16[6,32,128]{2,1,0:T(8,128)(2,1)S(1)}, u32[]{:S(2)}, u32[]{:S(2)}) collective-permute-start(bf16[6,32,128]{2,1,0:T(8,128)(2,1)S(1)} %pad_maximum_fusion.refs_2_), channel_id=1, source_target_pairs={{0,2},{1,3},{2,0},{3,1},{4,6},{5,7},{6,4},{7,5},{8,10},{9,11},{10,... | collective-permute-start | bytes 147464 | tf_op jit(solution)/shard_map/ppermute | solution.py:207
  7.1 5.2 %gather_fusion = bf16[1024,128]{1,0:T(8,128)(2,1)} fusion(bf16[2048,128]{1,0:T(8,128)(2,1)} %x_ref.1, s32[1024]{0:T(1024)S(1)} %broadcast_clamp_fusion), kind=kCustom, calls=%fused_computation | custom fusion | bytes 528384 | tf_op jit(solution)/shard_map/gather | solution.py:377
  12.3 6.1 %all-to-all-start = ((bf16[32,32,128]{2,1,0:T(8,128)(2,1)}), bf16[32,32,128]{2,1,0:T(8,128)(2,1)S(1)}, u32[]{:S(2)}, u32[]{:S(2)}) async-start(bf16[32,32,128]{2,1,0:T(8,128)(2,1)} %bitcast), calls=%async_computation | async-start | bytes 524288 | tf_op jit(solution)/shard_map/all_to_all | solution.py:378
  19.4 1.9 %copy.37 = f32[36,1024]{0,1:T(8,128)} copy(f32[36,1024]{1,0:T(8,128)} %param.14) | data formatting | bytes 294912 | tf_op args[3]
  23.3 11.0 %collective-permute-done.2.refs_4_ = bf16[32,128,128]{2,1,0:T(8,128)(2,1)S(1)} collective-permute-done((bf16[32,128,128]{2,1,0:T(8,128)(2,1)}, bf16[32,128,128]{2,1,0:T(8,128)(2,1)S(1)}, u32[]{:S(2)}, u32[]{:S(2)}) %collective-permute-start.2) | collective-permute-done | bytes 1048608 | tf_op jit(solution)/shard_map/ppermute | solution.py:206
  35.4 27.1 %shard_map.122 = (f32[2048,128]{1,0:T(8,128)}, bf16[1024,128]{1,0:T(8,128)(2,1)}) custom-call(s32[6,1024]{1,0:T(8,128)} %link_ref.1, s32[1]{0:T(128)S(6)} %copy.49.live_ref, bf16[2048,128]{1,0:T(8,128)(2,1)} %x_ref.1, bf16[1024,128]{1,0:T(8,128)(2,1)} %bitcast.63, f32[1024,36]{1,0:T(8,128)} %bitcast.62), custom_call_target="tpu_custom_call" | custom-call | flops 4000000000 | bytes 3145728 | tf_op jit(solution)/shard_map/pallas_call | solution.py:315
  62.5 5.3 %all-to-all-start.1 = ((bf16[32,32,128]{2,1,0:T(8,128)(2,1)}), bf16[32,32,128]{2,1,0:T(8,128)(2,1)}, u32[]{:S(2)}, u32[]{:S(2)}) async-start(bf16[32,32,128]{2,1,0:T(8,128)(2,1)} %bitcast.64), calls=%async_computation.1 | async-start | bytes 524288 | tf_op jit(solution)/shard_map/all_to_all | solution.py:387
  67.9 11.0 %shard_map.124.refs_6_ = f32[16,512,128]{2,1,0:T(8,128)} custom-call(s32[64]{0:T(128)S(1)} %fusion.41.refs_0_, f32[3,4]{1,0:T(4,128)S(1)} %copy-done.1, bf16[6,32,128]{2,1,0:T(8,128)(2,1)S(1)} %pad_maximum_fusion.refs_2_, bf16[6,32,128]{2,1,0:T(8,128)(2,1)S(1)} %collective-permute-done.4.refs_3_, bf16[32,128,128]{2,1,0:T(8,128)(2,1)S(1)} %copy-done, ...), custom_call_target="tpu_custom_call" | custom-call | flops 1073741824 | bytes 6291456 | tf_op jit(solution)/shard_map/pallas_call | solution.py:173
  78.9 12.2 %shard_map.125 = (f32[8,128,128]{2,1,0:T(8,128)S(1)}, f32[8,128,128]{2,1,0:T(8,128)S(1)}, f32[8,128,128]{2,1,0:T(8,128)S(1)}, f32[8,128,128]{2,1,0:T(8,128)S(1)}...) custom-call(s32[64]{0:T(128)S(1)} %fusion.42.refs_0_, ...), custom_call_target="tpu_custom_call" | custom-call | flops 1073741824 | bytes 6291456 | tf_op jit(solution)/shard_map/pallas_call | solution.py:173
  92.5 1.7 %collective-permute-start.6 = (bf16[8,128,128]{2,1,0:T(8,128)(2,1)}, bf16[8,128,128]{2,1,0:T(8,128)(2,1)S(1)}, u32[]{:S(2)}, u32[]{:S(2)}) collective-permute-start(bf16[8,128,128]{2,1,0:T(8,128)(2,1)} %get-tuple-element.15), channel_id=1, source_target_pairs={{0,4},{4,0},{8,12},{12,8},{16,20},{20,16},{24,28},{28,24},{1,5},{5... | collective-permute-start | bytes 786440 | tf_op jit(solution)/shard_map/ppermute | solution.py:234
  94.6 4.5 %shard_map.123 = f32[2048,128]{1,0:T(8,128)} custom-call(s32[1024]{0:T(1024)} %reshape.324.row_ref, bf16[1024,128]{1,0:T(8,128)(2,1)} %bitcast.4.back_ref, f32[2048,128]{1,0:T(8,128)} %get-tuple-element.13.own_ref), custom_call_target="tpu_custom_call" | custom-call | flops 1000000000 | bytes 2097152 | tf_op jit(solution)/shard_map/pallas_call | solution.py:360
  99.1 1.7 %collective-permute-start.12 = (bf16[8,128,128]{2,1,0:T(8,128)(2,1)}, bf16[8,128,128]{2,1,0:T(8,128)(2,1)S(1)}, u32[]{:S(2)}, u32[]{:S(2)}) collective-permute-start(bf16[8,128,128]{2,1,0:T(8,128)(2,1)} %copy-done.3), channel_id=1, source_target_pairs={{0,4},{4,0},{8,12},{12,8},{16,20},{20,16},{24,28},{28,24},{1,5},{5... | collective-permute-start | bytes 786440 | tf_op jit(solution)/shard_map/ppermute | solution.py:234
  102.0 1.8 %collective-permute-start.7 = (bf16[4,128,128]{2,1,0:T(8,128)(2,1)S(1)}, bf16[4,128,128]{2,1,0:T(8,128)(2,1)S(1)}, u32[]{:S(2)}, u32[]{:S(2)}) collective-permute-start(bf16[4,128,128]{2,1,0:T(8,128)(2,1)S(1)} %get-tuple-element.22), channel_id=1, source_target_pairs={{0,8},{4,12},{8,0},{12,4},{16,24},{20,28},{24,16},{28,20},{1,9},{5... | collective-permute-start | bytes 393224 | tf_op jit(solution)/shard_map/ppermute | solution.py:234
  103.7 3.8 %collective-permute-done.9 = bf16[8,128,128]{2,1,0:T(8,128)(2,1)S(1)} collective-permute-done((bf16[8,128,128]{2,1,0:T(8,128)(2,1)}, bf16[8,128,128]{2,1,0:T(8,128)(2,1)S(1)}, u32[]{:S(2)}, u32[]{:S(2)}) %collective-permute-start.9) | collective-permute-done | bytes 262176 | tf_op jit(solution)/shard_map/ppermute | solution.py:234
  107.6 1.8 %collective-permute-start.10 = (bf16[4,128,128]{2,1,0:T(8,128)(2,1)S(1)}, bf16[4,128,128]{2,1,0:T(8,128)(2,1)S(1)}, u32[]{:S(2)}, u32[]{:S(2)}) collective-permute-start(bf16[4,128,128]{2,1,0:T(8,128)(2,1)S(1)} %get-tuple-element.24), channel_id=1, source_target_pairs={{0,8},{4,12},{8,0},{12,4},{16,24},{20,28},{24,16},{28,20},{1,9},{5... | collective-permute-start | bytes 393224 | tf_op jit(solution)/shard_map/ppermute | solution.py:234
  109.3 3.8 %collective-permute-done.12 = bf16[8,128,128]{2,1,0:T(8,128)(2,1)S(1)} collective-permute-done((bf16[8,128,128]{2,1,0:T(8,128)(2,1)}, bf16[8,128,128]{2,1,0:T(8,128)(2,1)S(1)}, u32[]{:S(2)}, u32[]{:S(2)}) %collective-permute-start.12) | collective-permute-done | bytes 262176 | tf_op jit(solution)/shard_map/ppermute | solution.py:234
  113.2 1.8 %collective-permute-start.13 = (bf16[4,128,128]{2,1,0:T(8,128)(2,1)S(1)}, bf16[4,128,128]{2,1,0:T(8,128)(2,1)S(1)}, u32[]{:S(2)}, u32[]{:S(2)}) collective-permute-start(bf16[4,128,128]{2,1,0:T(8,128)(2,1)S(1)} %get-tuple-element.26), channel_id=1, source_target_pairs={{0,8},{4,12},{8,0},{12,4},{16,24},{20,28},{24,16},{28,20},{1,9},{5... | collective-permute-start | bytes 393224 | tf_op jit(solution)/shard_map/ppermute | solution.py:234
  115.0 3.0 %collective-permute-done.15 = bf16[8,128,128]{2,1,0:T(8,128)(2,1)S(1)} collective-permute-done((bf16[8,128,128]{2,1,0:T(8,128)(2,1)}, bf16[8,128,128]{2,1,0:T(8,128)(2,1)S(1)}, u32[]{:S(2)}, u32[]{:S(2)}) %collective-permute-start.15) | collective-permute-done | bytes 262176 | tf_op jit(solution)/shard_map/ppermute | solution.py:234
  118.0 1.7 %collective-permute-start.16 = (bf16[4,128,128]{2,1,0:T(8,128)(2,1)S(1)}, bf16[4,128,128]{2,1,0:T(8,128)(2,1)S(1)}, u32[]{:S(2)}, u32[]{:S(2)}) collective-permute-start(bf16[4,128,128]{2,1,0:T(8,128)(2,1)S(1)} %get-tuple-element.28), channel_id=1, source_target_pairs={{0,8},{4,12},{8,0},{12,4},{16,24},{20,28},{24,16},{28,20},{1,9},{5... | collective-permute-start | bytes 393224 | tf_op jit(solution)/shard_map/ppermute | solution.py:234
  119.8 2.5 %collective-permute-start.8 = (bf16[2,128,128]{2,1,0:T(8,128)(2,1)S(1)}, bf16[2,128,128]{2,1,0:T(8,128)(2,1)S(1)}, u32[]{:S(2)}, u32[]{:S(2)}) collective-permute-start(bf16[2,128,128]{2,1,0:T(8,128)(2,1)S(1)} %fusion.6), channel_id=1, source_target_pairs={{0,16},{4,20},{8,24},{12,28},{16,0},{20,4},{24,8},{28,12},{1,17},{... | collective-permute-start | bytes 196616 | tf_op jit(solution)/shard_map/ppermute | solution.py:234
  122.9 2.5 %collective-permute-start.14 = (bf16[2,128,128]{2,1,0:T(8,128)(2,1)S(1)}, bf16[2,128,128]{2,1,0:T(8,128)(2,1)S(1)}, u32[]{:S(2)}, u32[]{:S(2)}) collective-permute-start(bf16[2,128,128]{2,1,0:T(8,128)(2,1)S(1)} %fusion.2), channel_id=1, source_target_pairs={{0,16},{4,20},{8,24},{12,28},{16,0},{20,4},{24,8},{28,12},{1,17},{... | collective-permute-start | bytes 196616 | tf_op jit(solution)/shard_map/ppermute | solution.py:234
  125.4 1.7 %collective-permute-start.17 = (bf16[2,128,128]{2,1,0:T(8,128)(2,1)S(1)}, bf16[2,128,128]{2,1,0:T(8,128)(2,1)S(1)}, u32[]{:S(2)}, u32[]{:S(2)}) collective-permute-start(bf16[2,128,128]{2,1,0:T(8,128)(2,1)S(1)} %fusion), channel_id=1, source_target_pairs={{0,16},{4,20},{8,24},{12,28},{16,0},{20,4},{24,8},{28,12},{1,17},{... | collective-permute-start | bytes 196616 | tf_op jit(solution)/shard_map/ppermute | solution.py:234
  127.1 2.8 %collective-permute-done.8 = bf16[2,128,128]{2,1,0:T(8,128)(2,1)S(1)} collective-permute-done((bf16[2,128,128]{2,1,0:T(8,128)(2,1)S(1)}, bf16[2,128,128]{2,1,0:T(8,128)(2,1)S(1)}, u32[]{:S(2)}, u32[]{:S(2)}) %collective-permute-start.8) | collective-permute-done | bytes 65568 | tf_op jit(solution)/shard_map/ppermute | solution.py:234
  130.0 2.0 %collective-permute-done.11 = bf16[2,128,128]{2,1,0:T(8,128)(2,1)S(1)} collective-permute-done((bf16[2,128,128]{2,1,0:T(8,128)(2,1)S(1)}, bf16[2,128,128]{2,1,0:T(8,128)(2,1)S(1)}, u32[]{:S(2)}, u32[]{:S(2)}) %collective-permute-start.11) | collective-permute-done | bytes 65568 | tf_op jit(solution)/shard_map/ppermute | solution.py:234
  (82 shorter events, 14.3 us)
Async XLA Ops:
  2.8 19.9 %collective-permute-start.4 = (bf16[6,32,128]{2,1,0:T(8,128)(2,1)S(1)}, bf16[6,32,128]{2,1,0:T(8,128)(2,1)S(1)}, u32[]{:S(2)}, u32[]{:S(2)}) collective-permute-start(bf16[6,32,128]{2,1,0:T(8,128)(2,1)S(1)} %pad_maximum_fusion.refs_2_), channel_id=1, source_target_pairs={{0,1},{1,0},{2,3},{3,2},{4,5},{5,4},{6,7},{7,6},{8,9},{9,8},{10,11... | collective-permute-start | bytes 147464 | tf_op jit(solution)/shard_map/ppermute | solution.py:64
  3.3 19.7 %collective-permute-start = (bf16[6,32,128]{2,1,0:T(8,128)(2,1)S(1)}, bf16[6,32,128]{2,1,0:T(8,128)(2,1)S(1)}, u32[]{:S(2)}, u32[]{:S(2)}) collective-permute-start(bf16[6,32,128]{2,1,0:T(8,128)(2,1)S(1)} %pad_maximum_fusion.refs_2_), channel_id=1, source_target_pairs={{0,2},{1,3},{2,0},{3,1},{4,6},{5,7},{6,4},{7,5},{8,10},{9,11},{10,... | collective-permute-start | bytes 147464 | tf_op jit(solution)/shard_map/ppermute | solution.py:207
  5.9 62.0 %collective-permute-start.5 = (bf16[32,128,128]{2,1,0:T(8,128)(2,1)}, bf16[32,128,128]{2,1,0:T(8,128)(2,1)S(1)}, u32[]{:S(2)}, u32[]{:S(2)}) collective-permute-start(bf16[32,128,128]{2,1,0:T(8,128)(2,1)} %refs_4_.1), channel_id=1, source_target_pairs={{0,1},{1,0},{2,3},{3,2},{4,5},{5,4},{6,7},{7,6},{8,9},{9,8},{10,11... | collective-permute-start | bytes 3145736 | tf_op jit(solution)/shard_map/ppermute | solution.py:64
  6.0 28.3 %collective-permute-start.2 = (bf16[32,128,128]{2,1,0:T(8,128)(2,1)}, bf16[32,128,128]{2,1,0:T(8,128)(2,1)S(1)}, u32[]{:S(2)}, u32[]{:S(2)}) collective-permute-start(bf16[32,128,128]{2,1,0:T(8,128)(2,1)} %refs_4_.1), channel_id=1, source_target_pairs={{0,2},{1,3},{2,0},{3,1},{4,6},{5,7},{6,4},{7,5},{8,10},{9,11},{10,... | collective-permute-start | bytes 3145736 | tf_op jit(solution)/shard_map/ppermute | solution.py:206
  12.3 22.4 %all-to-all-start = ((bf16[32,32,128]{2,1,0:T(8,128)(2,1)}), bf16[32,32,128]{2,1,0:T(8,128)(2,1)S(1)}, u32[]{:S(2)}, u32[]{:S(2)}) async-start(bf16[32,32,128]{2,1,0:T(8,128)(2,1)} %bitcast), calls=%async_computation | async-start | bytes 524288 | tf_op jit(solution)/shard_map/all_to_all | solution.py:378
  23.0 11.4 %collective-permute-start.1 = (bf16[6,32,128]{2,1,0:T(8,128)(2,1)S(1)}, bf16[6,32,128]{2,1,0:T(8,128)(2,1)S(1)}, u32[]{:S(2)}, u32[]{:S(2)}) collective-permute-start(bf16[6,32,128]{2,1,0:T(8,128)(2,1)S(1)} %collective-permute-done.refs_2_), channel_id=1, source_target_pairs={{0,1},{1,0},{2,3},{3,2},{4,5},{5,4},{6,7},{7,6},{8,9},{9,8},{10,11... | collective-permute-start | bytes 147464 | tf_op jit(solution)/shard_map/ppermute | solution.py:64
  34.3 44.6 %collective-permute-start.3 = (bf16[32,128,128]{2,1,0:T(8,128)(2,1)S(1)}, bf16[32,128,128]{2,1,0:T(8,128)(2,1)}, u32[]{:S(2)}, u32[]{:S(2)}) collective-permute-start(bf16[32,128,128]{2,1,0:T(8,128)(2,1)S(1)} %collective-permute-done.2.refs_4_), channel_id=1, source_target_pairs={{0,1},{1,0},{2,3},{3,2},{4,5},{5,4},{6,7},{7,6},{8,9},{9,8},{10,11... | collective-permute-start | bytes 3145736 | tf_op jit(solution)/shard_map/ppermute | solution.py:64
  34.7 0.7 copy-start.4
  35.4 32.5 %copy-start = (bf16[32,128,128]{2,1,0:T(8,128)(2,1)S(1)}, bf16[32,128,128]{2,1,0:T(8,128)(2,1)}, u32[]{:S(2)}) copy-start(bf16[32,128,128]{2,1,0:T(8,128)(2,1)} %refs_4_.1) | copy-start | bytes 3145732
  35.4 32.5 %copy-start.1 = (f32[3,4]{1,0:T(4,128)S(1)}, f32[3,4]{1,0:T(4,128)}, u32[]{:S(2)}) copy-start(f32[3,4]{1,0:T(4,128)} %refs_1_.3) | copy-start | bytes 148
  62.5 32.0 %all-to-all-start.1 = ((bf16[32,32,128]{2,1,0:T(8,128)(2,1)}), bf16[32,32,128]{2,1,0:T(8,128)(2,1)}, u32[]{:S(2)}, u32[]{:S(2)}) async-start(bf16[32,32,128]{2,1,0:T(8,128)(2,1)} %bitcast.64), calls=%async_computation.1 | async-start | bytes 524288 | tf_op jit(solution)/shard_map/all_to_all | solution.py:387
  91.1 0.7 copy-start.2
  92.5 9.4 %collective-permute-start.6 = (bf16[8,128,128]{2,1,0:T(8,128)(2,1)}, bf16[8,128,128]{2,1,0:T(8,128)(2,1)S(1)}, u32[]{:S(2)}, u32[]{:S(2)}) collective-permute-start(bf16[8,128,128]{2,1,0:T(8,128)(2,1)} %get-tuple-element.15), channel_id=1, source_target_pairs={{0,4},{4,0},{8,12},{12,8},{16,20},{20,16},{24,28},{28,24},{1,5},{5... | collective-permute-start | bytes 786440 | tf_op jit(solution)/shard_map/ppermute | solution.py:234
  94.2 13.3 %collective-permute-start.9 = (bf16[8,128,128]{2,1,0:T(8,128)(2,1)}, bf16[8,128,128]{2,1,0:T(8,128)(2,1)S(1)}, u32[]{:S(2)}, u32[]{:S(2)}) collective-permute-start(bf16[8,128,128]{2,1,0:T(8,128)(2,1)} %get-tuple-element.17), channel_id=1, source_target_pairs={{0,4},{4,0},{8,12},{12,8},{16,20},{20,16},{24,28},{28,24},{1,5},{5... | collective-permute-start | bytes 786440 | tf_op jit(solution)/shard_map/ppermute | solution.py:234
  99.1 14.1 %collective-permute-start.12 = (bf16[8,128,128]{2,1,0:T(8,128)(2,1)}, bf16[8,128,128]{2,1,0:T(8,128)(2,1)S(1)}, u32[]{:S(2)}, u32[]{:S(2)}) collective-permute-start(bf16[8,128,128]{2,1,0:T(8,128)(2,1)} %copy-done.3), channel_id=1, source_target_pairs={{0,4},{4,0},{8,12},{12,8},{16,20},{20,16},{24,28},{28,24},{1,5},{5... | collective-permute-start | bytes 786440 | tf_op jit(solution)/shard_map/ppermute | solution.py:234
  100.8 17.2 %collective-permute-start.15 = (bf16[8,128,128]{2,1,0:T(8,128)(2,1)}, bf16[8,128,128]{2,1,0:T(8,128)(2,1)S(1)}, u32[]{:S(2)}, u32[]{:S(2)}) collective-permute-start(bf16[8,128,128]{2,1,0:T(8,128)(2,1)} %copy-done.2), channel_id=1, source_target_pairs={{0,4},{4,0},{8,12},{12,8},{16,20},{20,16},{24,28},{28,24},{1,5},{5... | collective-permute-start | bytes 786440 | tf_op jit(solution)/shard_map/ppermute | solution.py:234
  102.0 17.8 %collective-permute-start.7 = (bf16[4,128,128]{2,1,0:T(8,128)(2,1)S(1)}, bf16[4,128,128]{2,1,0:T(8,128)(2,1)S(1)}, u32[]{:S(2)}, u32[]{:S(2)}) collective-permute-start(bf16[4,128,128]{2,1,0:T(8,128)(2,1)S(1)} %get-tuple-element.22), channel_id=1, source_target_pairs={{0,8},{4,12},{8,0},{12,4},{16,24},{20,28},{24,16},{28,20},{1,9},{5... | collective-permute-start | bytes 393224 | tf_op jit(solution)/shard_map/ppermute | solution.py:234
  107.6 14.7 %collective-permute-start.10 = (bf16[4,128,128]{2,1,0:T(8,128)(2,1)S(1)}, bf16[4,128,128]{2,1,0:T(8,128)(2,1)S(1)}, u32[]{:S(2)}, u32[]{:S(2)}) collective-permute-start(bf16[4,128,128]{2,1,0:T(8,128)(2,1)S(1)} %get-tuple-element.24), channel_id=1, source_target_pairs={{0,8},{4,12},{8,0},{12,4},{16,24},{20,28},{24,16},{28,20},{1,9},{5... | collective-permute-start | bytes 393224 | tf_op jit(solution)/shard_map/ppermute | solution.py:234
  113.2 9.6 %collective-permute-start.13 = (bf16[4,128,128]{2,1,0:T(8,128)(2,1)S(1)}, bf16[4,128,128]{2,1,0:T(8,128)(2,1)S(1)}, u32[]{:S(2)}, u32[]{:S(2)}) collective-permute-start(bf16[4,128,128]{2,1,0:T(8,128)(2,1)S(1)} %get-tuple-element.26), channel_id=1, source_target_pairs={{0,8},{4,12},{8,0},{12,4},{16,24},{20,28},{24,16},{28,20},{1,9},{5... | collective-permute-start | bytes 393224 | tf_op jit(solution)/shard_map/ppermute | solution.py:234
  118.0 7.3 %collective-permute-start.16 = (bf16[4,128,128]{2,1,0:T(8,128)(2,1)S(1)}, bf16[4,128,128]{2,1,0:T(8,128)(2,1)S(1)}, u32[]{:S(2)}, u32[]{:S(2)}) collective-permute-start(bf16[4,128,128]{2,1,0:T(8,128)(2,1)S(1)} %get-tuple-element.28), channel_id=1, source_target_pairs={{0,8},{4,12},{8,0},{12,4},{16,24},{20,28},{24,16},{28,20},{1,9},{5... | collective-permute-start | bytes 393224 | tf_op jit(solution)/shard_map/ppermute | solution.py:234
  119.8 10.1 %collective-permute-start.8 = (bf16[2,128,128]{2,1,0:T(8,128)(2,1)S(1)}, bf16[2,128,128]{2,1,0:T(8,128)(2,1)S(1)}, u32[]{:S(2)}, u32[]{:S(2)}) collective-permute-start(bf16[2,128,128]{2,1,0:T(8,128)(2,1)S(1)} %fusion.6), channel_id=1, source_target_pairs={{0,16},{4,20},{8,24},{12,28},{16,0},{20,4},{24,8},{28,12},{1,17},{... | collective-permute-start | bytes 196616 | tf_op jit(solution)/shard_map/ppermute | solution.py:234
  122.3 9.7 %collective-permute-start.11 = (bf16[2,128,128]{2,1,0:T(8,128)(2,1)S(1)}, bf16[2,128,128]{2,1,0:T(8,128)(2,1)S(1)}, u32[]{:S(2)}, u32[]{:S(2)}) collective-permute-start(bf16[2,128,128]{2,1,0:T(8,128)(2,1)S(1)} %fusion.4), channel_id=1, source_target_pairs={{0,16},{4,20},{8,24},{12,28},{16,0},{20,4},{24,8},{28,12},{1,17},{... | collective-permute-start | bytes 196616 | tf_op jit(solution)/shard_map/ppermute | solution.py:234
  122.9 10.5 %collective-permute-start.14 = (bf16[2,128,128]{2,1,0:T(8,128)(2,1)S(1)}, bf16[2,128,128]{2,1,0:T(8,128)(2,1)S(1)}, u32[]{:S(2)}, u32[]{:S(2)}) collective-permute-start(bf16[2,128,128]{2,1,0:T(8,128)(2,1)S(1)} %fusion.2), channel_id=1, source_target_pairs={{0,16},{4,20},{8,24},{12,28},{16,0},{20,4},{24,8},{28,12},{1,17},{... | collective-permute-start | bytes 196616 | tf_op jit(solution)/shard_map/ppermute | solution.py:234
  125.4 8.8 %collective-permute-start.17 = (bf16[2,128,128]{2,1,0:T(8,128)(2,1)S(1)}, bf16[2,128,128]{2,1,0:T(8,128)(2,1)S(1)}, u32[]{:S(2)}, u32[]{:S(2)}) collective-permute-start(bf16[2,128,128]{2,1,0:T(8,128)(2,1)S(1)} %fusion), channel_id=1, source_target_pairs={{0,16},{4,20},{8,24},{12,28},{16,0},{20,4},{24,8},{28,12},{1,17},{... | collective-permute-start | bytes 196616 | tf_op jit(solution)/shard_map/ppermute | solution.py:234
  (1 other events, 0.7 us)

commit v2 on v1

v2 whole, which is shorter than its diff:
```python
import math

import jax
import jax.numpy as jnp
from jax import lax
from jax.experimental import pallas as pl
from jax.experimental.pallas import tpu as pltpu
from jax.sharding import PartitionSpec as P

LEAVES_DEV = 16
OCTANTS = 8
NODES = 4
PLANE = NODES * NODES
SQUARE = NODES**3
POINTS = [math.cos((2 * j + 1) * math.pi / (2 * NODES)) for j in range(NODES)]
MESH = pl.DeviceIdType.MESH
VMEM = pl.BlockSpec(memory_space=pltpu.VMEM)
SMEM = pl.BlockSpec(memory_space=pltpu.SMEM)


def lagrange_rows(v):
    rows = []
    for target in range(NODES):
        product = None
        scale = 1.0
        for other in range(NODES):
            if other != target:
                factor = v - POINTS[other]
                product = factor if product is None else product * factor
                scale *= POINTS[target] - POINTS[other]
        rows.append(product * (1.0 / scale))
    return rows


def cos_sin(phase):
    turns = jnp.floor(phase * (1.0 / math.pi) + 0.5)
    odd = turns - 2.0 * jnp.floor(turns * 0.5)
    sign = 1.0 - 2.0 * odd
    high = 3.140625
    rest = (phase - turns * high) - turns * (math.pi - high)
    square = rest * rest
    cosine = jnp.full_like(rest, 1.0 / math.factorial(12))
    for order in (10, 8, 6, 4, 2, 0):
        cosine = cosine * square + (1.0 if order % 4 == 0 else -1.0) / math.factorial(order)
    sine = jnp.full_like(rest, -1.0 / math.factorial(11))
    for order in (9, 7, 5, 3, 1):
        sine = sine * square + (1.0 if order % 4 == 1 else -1.0) / math.factorial(order)
    return cosine * sign, sine * rest * sign


def xor_pairs(count, bit):
    return [(i, i ^ (1 << bit)) for i in range(count)]


def log2(count):
    bits = count.bit_length() - 1
    if count != 1 << bits:
        raise ValueError("axis size")
    return bits


def spread(value, axis, bits):
    held = [value]
    count = lax.axis_size(axis)
    for bit in bits:
        held = held + [lax.ppermute(h, axis, xor_pairs(count, bit)) for h in held]
    return held


def block_sums(waves, numbers, places, blocks, previous, slot_count, cone_count):
    last = previous is not None
    units = 2 * cone_count
    lists = len(blocks)
    per_list, block_size, columns = blocks[0].shape
    total = lists * per_list
    height = units * SQUARE
    firsts = units * NODES
    rows = PLANE + firsts
    group = 16
    place_rows = 8
    half = slot_count // 2
    parents = LEAVES_DEV // OCTANTS

    def kernel(*refs):
        wave_ref = refs[0]
        number_refs = refs[1 : 1 + lists]
        place_refs = refs[1 + lists : 1 + 2 * lists]
        block_refs = refs[1 + 2 * lists : 1 + 3 * lists]
        at = 1 + 3 * lists
        if last:
            before_ref, keep_ref, send_ref, sum_ref = refs[at : at + 4]
        else:
            sum_ref = refs[at]
        factor_ref, place_ref, number_ref = refs[-3:]

        for which in range(lists):

            def unpack(index, carry):
                at_block = which * per_list + index
                place = place_refs[which][index].astype(jnp.float32)
                place_ref[pl.ds(pl.multiple_of(at_block * place_rows, place_rows), 3), :] = place
                leaf = number_refs[which][0, index]
                shifts = [(leaf >> 2) & 1, (leaf >> 1) & 1, leaf & 1]
                values = [(2 * shift - 1).astype(jnp.float32) for shift in shifts]
                values.append(number_refs[which][1, index].astype(jnp.float32))
                for row, value in enumerate(values):
                    number_ref[row, pl.ds(at_block, 1), :] = jnp.full(
                        (1, block_size), value, jnp.float32
                    )
                return carry

            lax.fori_loop(0, per_list, unpack, 0, unroll=4)

        lanes = lax.broadcasted_iota(jnp.int32, (group, block_size), 1).astype(jnp.float32)
        for part in range(total // group):
            span = pl.ds(part * group, group)
            double = [
                number_ref[d, span, :]
                + place_ref[pl.ds(part * group * place_rows + d, group, stride=place_rows), :]
                for d in range(3)
            ]
            live = lanes < number_ref[3, span, :]
            first = [jnp.where(live, r, 0.0) for r in lagrange_rows(0.5 * double[0])]
            second = lagrange_rows(0.5 * double[1])
            third = lagrange_rows(0.5 * double[2])
            start = part * group * rows

            def put(row, value):
                factor_ref[pl.ds(start + row, group, stride=rows), :] = value

            for a in range(NODES):
                for b in range(NODES):
                    put(a * NODES + b, second[a] * third[b])
            for cone in range(cone_count):
                phase = (
                    wave_ref[0, cone] * double[0]
                    + wave_ref[1, cone] * double[1]
                    + wave_ref[2, cone] * double[2]
                )
                cosine, sine = cos_sin(phase)
                for digit in range(NODES):
                    put(PLANE + cone * 2 * NODES + digit, first[digit] * cosine)
                    put(PLANE + cone * 2 * NODES + NODES + digit, first[digit] * -sine)

        sum_ref[...] = jnp.zeros_like(sum_ref)
        me = lax.axis_index("dom")
        bits = log2(lax.axis_size("dom"))

        def slot_of(which, index):
            leaf, owner = number_refs[which][0, index], number_refs[which][2, index]
            relative = owner ^ me
            order = leaf >> 3
            for bit in range(bits):
                order = order + (((relative >> bit) & 1) << (bits - 1 - bit)) * parents
            return order

        def weights_of(index):
            base = pl.multiple_of(index * rows, 8)
            pairs = factor_ref[pl.ds(base, PLANE), :]
            pieces = [
                (factor_ref[pl.ds(base + PLANE + row, 1), :] * pairs).astype(jnp.bfloat16)
                for row in range(firsts)
            ]
            return jnp.concatenate(pieces, axis=0)

        empty = jnp.zeros((block_size, columns), jnp.bfloat16)
        for which in range(lists):
            def two(pair, carry):
                index = which * per_list + 2 * pair
                weights = jnp.concatenate([weights_of(index), weights_of(index + 1)], axis=1)
                wide = jnp.concatenate(
                    [
                        jnp.concatenate([block_refs[which][2 * pair], empty], axis=1),
                        jnp.concatenate([empty, block_refs[which][2 * pair + 1]], axis=1),
                    ],
                    axis=0,
                )
                product = jnp.dot(weights, wide, preferred_element_type=jnp.float32)
                sum_ref[slot_of(which, 2 * pair)] += product[:, :columns]
                sum_ref[slot_of(which, 2 * pair + 1)] += product[:, columns:]
                return carry

            lax.fori_loop(0, per_list // 2, two, 0)

        if last:

            def finish(slot, carry):
                for unit in range(units):
                    span = pl.ds(unit * SQUARE, SQUARE)
                    keep_ref[unit, slot] = sum_ref[slot, span, :] + before_ref[slot, span, :]
                    send_ref[unit, slot] = (
                        sum_ref[half + slot, span, :] + before_ref[half + slot, span, :]
                    ).astype(jnp.bfloat16)
                return carry

            lax.fori_loop(0, half, finish, 0)

    whole = (slot_count, height, columns)
    scratch = [
        pltpu.VMEM((total * rows, block_size), jnp.float32),
        pltpu.VMEM((total * place_rows, block_size), jnp.float32),
        pltpu.VMEM((4, total, block_size), jnp.float32),
    ]
    out_shape = [jax.ShapeDtypeStruct(whole, jnp.float32)]
    if last:
        split = (units, half, SQUARE, columns)
        out_shape = [
            jax.ShapeDtypeStruct(split, jnp.float32),
            jax.ShapeDtypeStruct(split, jnp.bfloat16),
        ]
        scratch = [pltpu.VMEM(whole, jnp.float32)] + scratch
    operands = [waves, *numbers, *places, *blocks] + ([previous] if last else [])
    need = 3 * slot_count * height * columns * 4 + total * (rows + 12 + 64) * block_size * 4
    return pl.pallas_call(
        kernel,
        out_shape=out_shape,
        in_specs=[SMEM] * (1 + lists) + [VMEM] * (2 * lists + last),
        out_specs=[VMEM] * len(out_shape),
        scratch_shapes=scratch,
        compiler_params=pltpu.CompilerParams(vmem_limit_bytes=min(need + (3 << 20), 60 << 20)),
        cost_estimate=pl.CostEstimate(
            flops=2 * total * height * block_size * columns,
            bytes_accessed=total * block_size * columns * 2 + slot_count * height * columns * 4,
            transcendentals=0,
        ),
    )(*operands)


def rotate(sums, cone_waves):
    parents, units, square, columns = sums.shape
    cone_count = cone_waves.shape[1]
    digits = jnp.arange(square)
    digits = jnp.stack([digits // PLANE, digits // NODES % NODES, digits % NODES])
    nodes = jnp.cos((2.0 * digits.astype(jnp.float32) + 1.0) * (math.pi / (2.0 * NODES)))
    angle = 2.0 * (
        cone_waves[0][:, None] * nodes[0]
        + cone_waves[1][:, None] * nodes[1]
        + cone_waves[2][:, None] * nodes[2]
    )
    cosine, sine = jnp.cos(angle)[None, :, :, None], jnp.sin(angle)[None, :, :, None]
    parts = sums.reshape(parents, cone_count, 2, square, columns)
    real, imag = parts[:, :, 0], parts[:, :, 1]
    return jnp.stack([cosine * real - sine * imag, cosine * imag + sine * real], axis=2)


def mesh_flat():
    dirs = lax.axis_size("dir")
    return lax.axis_index("dom") * dirs + lax.axis_index("dir"), lax.axis_size("dom") * dirs


def greet_all():
    me, count = mesh_flat()
    dirs = lax.axis_size("dir")
    barrier = pltpu.get_barrier_semaphore()

    def one(offset, carry):
        peer = (me + offset) % count
        pl.semaphore_signal(
            barrier, inc=1, device_id=(peer // dirs, peer % dirs), device_id_type=MESH
        )
        return carry

    lax.fori_loop(1, count, one, 0)
    return barrier, count - 1


def send_rows(source, landing, width, send_sem, recv_sem):
    me, count = mesh_flat()
    dirs = lax.axis_size("dir")

    def one(offset, carry):
        peer = (me + offset) % count
        pltpu.make_async_remote_copy(
            src_ref=source.at[pl.ds(pl.multiple_of(peer * width, width), width)],
            dst_ref=landing.at[pl.ds(pl.multiple_of(me * width, width), width)],
            send_sem=send_sem,
            recv_sem=recv_sem,
            device_id=(peer // dirs, peer % dirs),
            device_id_type=MESH,
        ).start()
        return carry

    lax.fori_loop(1, count, one, 0)
    span = pl.ds(0, (count - 1) * width)
    peer = (me + 1) % count
    return pltpu.make_async_remote_copy(
        src_ref=source.at[span],
        dst_ref=landing.at[span],
        send_sem=send_sem,
        recv_sem=recv_sem,
        device_id=(peer // dirs, peer % dirs),
        device_id_type=MESH,
    )


def halo_rows(x_edges, send_list):
    owned_rows, columns = x_edges.shape
    partitions, width = send_list.shape

    def kernel(list_ref, x_ref, out_ref, table_ref, got_ref, send_ref, send_sem, recv_sem):
        barrier, others = greet_all()
        me, _ = mesh_flat()
        table_ref[...] = x_ref[...].astype(jnp.float32)

        def one(part, carry):
            start = pl.multiple_of(part * width, width)
            for lane in range(width):
                row = jnp.minimum(list_ref[part, lane], owned_rows - 1)
                got_ref[pl.ds(start + lane, 1), :] = table_ref[pl.ds(row, 1), :]
            return carry

        lax.fori_loop(0, partitions, one, 0)
        send_ref[...] = got_ref[...].astype(jnp.bfloat16)
        own = pl.ds(pl.multiple_of(me * width, width), width)
        out_ref[own, :] = jnp.zeros((width, columns), jnp.bfloat16)
        pl.semaphore_wait(barrier, others)
        whole = send_rows(send_ref, out_ref, width, send_sem, recv_sem)
        whole.wait_send()
        whole.wait_recv()

    return pl.pallas_call(
        kernel,
        out_shape=jax.ShapeDtypeStruct((partitions * width, columns), jnp.bfloat16),
        in_specs=[SMEM, VMEM],
        out_specs=VMEM,
        scratch_shapes=[
            pltpu.VMEM((owned_rows, columns), jnp.float32),
            pltpu.VMEM((partitions * width, columns), jnp.float32),
            pltpu.VMEM((partitions * width, columns), jnp.bfloat16),
            pltpu.SemaphoreType.DMA,
            pltpu.SemaphoreType.DMA,
        ],
        compiler_params=pltpu.CompilerParams(
            collective_id=0, has_side_effects=True, vmem_limit_bytes=16 << 20
        ),
        cost_estimate=pl.CostEstimate(
            flops=1_000_000_000, bytes_accessed=owned_rows * columns * 2, transcendentals=0
        ),
    )(send_list, x_edges)


def element_sums(links, live, x_edges, received, mats):
    element_count = mats.shape[1]
    edges = links.shape[0] // element_count
    owned_rows, columns = x_edges.shape
    halo = received.shape[0]
    table_rows = owned_rows + halo
    step = 8
    wide = 128

    def kernel(link_ref, live_ref, x_ref, halo_ref, mat_ref, own_ref, back_ref, *scratch):
        table_ref, term_ref = scratch[:2]
        got_refs, sums = scratch[2:4], scratch[4:]
        table_ref[pl.ds(0, owned_rows), :] = x_ref[...].astype(jnp.float32)
        table_ref[pl.ds(owned_rows, halo), :] = halo_ref[...].astype(jnp.float32)
        for ref in sums:
            ref[...] = jnp.zeros_like(ref)
        here = lax.broadcasted_iota(jnp.int32, (wide, wide), 0)
        there = lax.broadcasted_iota(jnp.int32, (wide, wide), 1)
        eye = jnp.where(here == there, 1.0, 0.0).astype(jnp.bfloat16)

        def fetch(number, got_ref):
            start = pl.multiple_of(number * wide, wide)
            for edge in range(edges):
                for lane in range(wide):
                    row = link_ref[start + (edge * element_count + lane)]
                    got_ref[pl.ds(edge * wide + lane, 1), :] = table_ref[pl.ds(row, 1), :]

        def product(number, got_ref):
            start = pl.multiple_of(number * wide, wide)
            count = start + lax.broadcasted_iota(jnp.int32, (1, wide), 1)
            live = count < live_ref[0]
            got = got_ref[...].astype(jnp.bfloat16)
            for i in range(edges):
                diagonals = []
                for j in range(edges):
                    row = mat_ref[pl.ds(edges * i + j, 1), pl.ds(start, wide)]
                    row = jnp.where(live, row, 0.0).astype(jnp.bfloat16)
                    diagonals.append(eye * row)
                term_ref[i, pl.ds(start, wide), :] = jnp.dot(
                    jnp.concatenate(diagonals, axis=1), got, preferred_element_type=jnp.float32
                )

        tiles = element_count // wide

        def products(index, carry):
            fetch(2 * index + 1, got_refs[1])
            product(2 * index, got_refs[0])
            fetch(jnp.minimum(2 * index + 2, tiles - 1), got_refs[0])
            product(2 * index + 1, got_refs[1])
            return carry

        fetch(0, got_refs[0])
        lax.fori_loop(0, tiles // 2, products, 0)

        def scatter(number, carry):
            start = pl.multiple_of(number * step, step)
            for lane in range(step):
                for edge in range(edges):
                    row = link_ref[start + (edge * element_count + lane)]
                    sums[edge][pl.ds(row, 1), :] += term_ref[edge, pl.ds(start + lane, 1), :]
            return carry

        lax.fori_loop(0, element_count // step, scatter, 0, unroll=2)

        def total_of(span):
            total = sums[0][span, :]
            for ref in sums[1:]:
                total = total + ref[span, :]
            return total

        own_ref[...] = total_of(pl.ds(0, owned_rows))
        back_ref[...] = total_of(pl.ds(owned_rows, halo)).astype(jnp.bfloat16)

    need = (edges + 4) * table_rows * columns * 4 + (6 << 20)
    return pl.pallas_call(
        kernel,
        out_shape=[
            jax.ShapeDtypeStruct((owned_rows, columns), jnp.float32),
            jax.ShapeDtypeStruct((halo, columns), jnp.bfloat16),
        ],
        in_specs=[SMEM, SMEM, VMEM, VMEM, VMEM],
        out_specs=[VMEM, VMEM],
        scratch_shapes=[
            pltpu.VMEM((table_rows, columns), jnp.float32),
            pltpu.VMEM((edges, element_count, columns), jnp.float32),
            pltpu.VMEM((edges * wide, columns), jnp.float32),
            pltpu.VMEM((edges * wide, columns), jnp.float32),
        ]
        + [pltpu.VMEM((table_rows, columns), jnp.float32)] * edges,
        compiler_params=pltpu.CompilerParams(vmem_limit_bytes=need),
        cost_estimate=pl.CostEstimate(
            flops=4_000_000_000, bytes_accessed=table_rows * columns * 8, transcendentals=0
        ),
    )(links, live, x_edges, received, mats)


def return_and_reduce(back, rows, keep, send, owned_rows, parents):
    partitions = lax.axis_size("dom") * lax.axis_size("dir")
    total_rows, columns = back.shape
    width = total_rows // partitions
    units, half, height, _ = keep.shape
    steps = log2(lax.axis_size("dom"))
    sizes = [half >> k for k in range(steps)]
    fold_step = 256

    def kernel(row_ref, back_ref, keep_ref, send_ref, fold_ref, out_ref, *scratch):
        land_ref = scratch[0]
        got = scratch[1 : 1 + steps]
        keeps = [keep_ref] + list(scratch[1 + steps : 2 * steps])
        sends = [send_ref] + list(scratch[2 * steps : 3 * steps - 1])
        back_send, back_recv, send_sems, recv_sems = scratch[3 * steps - 1 :]
        me, _ = mesh_flat()
        dom = lax.axis_index("dom")
        barrier, others = greet_all()
        own = pl.ds(pl.multiple_of(me * width, width), width)
        land_ref[own, :] = jnp.zeros((width, columns), jnp.bfloat16)
        pl.semaphore_wait(barrier, others)
        def copy(k, unit):
            bit = 1 << k
            partner = dom + bit * (1 - 2 * ((dom // bit) % 2))
            return pltpu.make_async_remote_copy(
                src_ref=sends[k].at[unit],
                dst_ref=got[k].at[unit],
                send_sem=send_sems.at[k, unit],
                recv_sem=recv_sems.at[k, unit],
                device_id=(partner, lax.axis_index("dir")),
                device_id_type=MESH,
            )

        for unit in range(units):
            copy(0, unit).start()
        whole = send_rows(back_ref, land_ref, width, back_send, back_recv)

        def fold_all():
            whole.wait_recv()
            landed = land_ref[...]
            listed = row_ref[...]

            def fold(index, carry):
                start = pl.multiple_of(index * fold_step, fold_step)
                mine = start + lax.broadcasted_iota(jnp.int32, (fold_step, total_rows), 0)
                picks = jnp.where(mine == listed, 1.0, 0.0).astype(jnp.bfloat16)
                fold_ref[pl.ds(start, fold_step), :] = jnp.dot(
                    picks, landed, preferred_element_type=jnp.float32
                )
                return carry

            lax.fori_loop(0, owned_rows // fold_step, fold, 0)

        for turn in range(units + steps - 1):
            if turn == units:
                fold_all()
            for k in range(steps):
                unit = turn - k
                if not 0 <= unit < units:
                    continue
                copy(k, unit).wait_recv()
                if k < steps - 1:
                    low = sizes[k + 1]
                    upper, lower = pl.ds(low, low), pl.ds(0, low)
                    sends[k + 1][unit] = (
                        keeps[k][unit, upper] + got[k][unit, upper].astype(jnp.float32)
                    ).astype(jnp.bfloat16)
                    copy(k + 1, unit).start()
                    keeps[k + 1][unit] = keeps[k][unit, lower] + got[k][unit, lower].astype(
                        jnp.float32
                    )
                else:
                    for parent in range(parents):
                        out_ref[parent, unit] = keeps[k][unit, parent] + got[k][
                            unit, parent
                        ].astype(jnp.float32)
        whole.wait_send()
        for k in range(steps):
            for unit in range(units):
                copy(k, unit).wait_send()

    def buffers(dtype, first):
        return [pltpu.VMEM((units, size, height, columns), dtype) for size in sizes[first:]]

    scratch = (
        [pltpu.VMEM((total_rows, columns), jnp.bfloat16)]
        + buffers(jnp.bfloat16, 0)
        + buffers(jnp.float32, 1)
        + buffers(jnp.bfloat16, 1)
    )
    need = half * units * height * columns * 16 + total_rows * columns * 16 + (8 << 20)
    return pl.pallas_call(
        kernel,
        out_shape=[
            jax.ShapeDtypeStruct((owned_rows, columns), jnp.float32),
            jax.ShapeDtypeStruct((parents, units, height, columns), jnp.float32),
        ],
        in_specs=[VMEM] * 4,
        out_specs=[VMEM, VMEM],
        scratch_shapes=scratch
        + [
            pltpu.SemaphoreType.DMA,
            pltpu.SemaphoreType.DMA,
            pltpu.SemaphoreType.DMA((steps, units)),
            pltpu.SemaphoreType.DMA((steps, units)),
        ],
        compiler_params=pltpu.CompilerParams(
            collective_id=1, has_side_effects=True, vmem_limit_bytes=min(need, 60 << 20)
        ),
        cost_estimate=pl.CostEstimate(
            flops=2 * owned_rows * total_rows * columns,
            bytes_accessed=half * units * height * columns * 6,
            transcendentals=0,
        ),
    )(rows, back, keep, send)


def shards(
    x_edges,
    send_list,
    connectivity,
    elem_mats,
    elem_live,
    currents,
    positions,
    block_live,
    block_owner,
    block_leaf,
    cone_waves,
):
    dom_count, dir_count = lax.axis_size("dom"), lax.axis_size("dir")
    parents = LEAVES_DEV // OCTANTS
    slot_count = dom_count * parents
    dir_bits = log2(dir_count)
    cone_count = cone_waves.shape[1]
    owned_rows = x_edges.shape[0]

    numbers = jnp.stack([block_leaf, block_live, block_owner])
    own = (numbers, positions, currents)
    near_bits = list(range(dir_bits - 1))
    near = [spread(value, "dir", near_bits) for value in own]
    received = halo_rows(x_edges, send_list)
    late, received = lax.optimization_barrier((currents, received))
    own = (numbers, positions, late)
    far = [lax.ppermute(value, "dir", xor_pairs(dir_count, dir_bits - 1)) for value in own]
    owned, back = element_sums(connectivity.reshape(-1), elem_live, x_edges, received, elem_mats)
    (sums,) = block_sums(cone_waves, *near, None, slot_count, cone_count)
    *far, back = lax.optimization_barrier((*far, back))
    far = [spread(value, "dir", near_bits) for value in far]
    keep, send = block_sums(cone_waves, *far, sums, slot_count, cone_count)
    fold, sums = return_and_reduce(
        back, send_list.reshape(1, -1), keep, send, owned_rows, parents
    )
    return owned + fold, rotate(sums, cone_waves)


def solution(mesh):
    placed = (
        P(("dom", "dir"), None),
        P(("dom", "dir"), None),
        P(None, ("dom", "dir")),
        P(None, ("dom", "dir")),
        P(("dom", "dir")),
        P(("dom", "dir"), None, None),
        P(("dom", "dir"), None, None),
        P(("dom", "dir")),
        P(("dom", "dir")),
        P(("dom", "dir")),
        P(None, "dir"),
    )
    return jax.shard_map(
        shards,
        mesh=mesh,
        in_specs=placed,
        out_specs=(P(("dom", "dir"), None), P("dom", "dir", None, None, None)),
        check_vma=False,
    )
```

time: 136 us -> 109 us (0.80)
  Pallas kernels: 54.8 us -> 91.1 us
  waiting for transfers between devices: 29.2 us -> 0.64 us
  starting transfers between devices: 33.5 us -> 5.17 us
  local copies, waits for them, and re-layouts: 11.5 us -> 6.97 us
  other arithmetic: 4.68 us -> 2.99 us
    pallas_call x3 -> x4, Pallas kernels: 27.7 us -> 75.4 us  [the longest x1 40.4 us: return_and_reduce(): pl.pallas_call(kernel, out_shape=[jax.ShapeDtypeStruct((owned_rows, colum...]
    ppermute x14 -> x3, waiting for transfers between devices: 29.2 us -> 0.37 us  [shards(): lax.ppermute(value, 'dir', xor_pairs(dir_count, dir_bits - 1))]
    ppermute x14 -> x3, starting transfers between devices: 21.1 us -> 3.89 us  [shards(): lax.ppermute(value, 'dir', xor_pairs(dir_count, dir_bits - 1))]
    all_to_all x2 -> x0, starting transfers between devices: 11.4 us -> none  [the longest x1 6.07 us: interior_part(): lax.all_to_all(outgoing, ('dom', 'dir'), split_axis=0, concat_axis=0, til...]
    pallas_call x1, Pallas kernels: 27.1 us -> 15.7 us  [element_sums(): pl.pallas_call(kernel, out_shape=[jax.ShapeDtypeStruct((owned_rows, colum...]
    gather x1 -> x0, local copies, waits for them, and re-layouts: 5.19 us -> none  [interior_part(): outgoing = x_edges[rows]]
    unnamed x11 -> x19, local copies, waits for them, and re-layouts: 4.03 us -> 6.12 us
    concatenate x2 -> x0, other arithmetic: 1.58 us -> none  [the longest x1 0.83 us: boundary_part(): return jnp.concatenate(outs, axis=1)]
  transfers between devices with their start and end apart: 20 -> 9, of which waited for: 9 -> 2; matrix products, arithmetic and copies ran while one was open for 8% -> 2% of each run, Pallas kernels for 41% -> 24%
where the time goes in v2:
time: 109 us; the launch traced here: 108 us
  Pallas kernels  91.1 us (84%)
  local copies, waits for them, and re-layouts  6.97 us (6%)
  starting transfers between devices  5.17 us (5%)
  other arithmetic  2.99 us (3%)
  between operations  1.43 us (1%)
    pallas_call x1, Pallas kernels, return_and_reduce(): pl.pallas_call(kernel, out_shape=[jax.ShapeDtypeStruct((owned_rows, colum...  40.4 us
    pallas_call x2, Pallas kernels, block_sums(): pl.pallas_call(kernel, out_shape=out_shape, in_specs=[SMEM] * (1 + lists)...  21.9 us
    pallas_call x1, Pallas kernels, element_sums(): pl.pallas_call(kernel, out_shape=[jax.ShapeDtypeStruct((owned_rows, colum...  15.7 us
    pallas_call x1, Pallas kernels, halo_rows(): pl.pallas_call(kernel, out_shape=jax.ShapeDtypeStruct((partitions * width...  13.1 us
    unnamed x19, local copies, waits for them, and re-layouts  6.12 us
    ppermute x3, starting transfers between devices, shards(): lax.ppermute(value, 'dir', xor_pairs(dir_count, dir_bits - 1))  3.89 us
  transfers between devices with their start and end apart: 9, of which 2 were waited for; matrix products, arithmetic and copies ran while one was open for 2% of the time, Pallas kernels for 24%

profile of v2, /device:TPU:0, one launch (start us, length us, event | category | flops | bytes accessed | tf_op | source)
XLA Modules:
  0.0 108.3 jit_solution(8797882071982579080)
XLA Ops:
  0.6 0.7 copy-done.1
  1.4 1.0 copy-done.4
  2.4 13.1 %shard_map.122.halo_ref = bf16[1024,128]{1,0:T(8,128)(2,1)S(1)} custom-call(s32[32,32]{1,0:T(8,128)S(1)} %copy-done.1, bf16[2048,128]{1,0:T(8,128)(2,1)S(1)} %copy-done.4), custom_call_target="tpu_custom_call" | custom-call | flops 1000000000 | bytes 524288 | tf_op jit(solution)/shard_map/pallas_call | solution.py:321
  15.5 0.7 copy-done.7
  16.2 1.8 %collective-permute-start.2 = (bf16[32,128,128]{2,1,0:T(8,128)(2,1)}, bf16[32,128,128]{2,1,0:T(8,128)(2,1)S(1)}, u32[]{:S(2)}, u32[]{:S(2)}) collective-permute-start(bf16[32,128,128]{2,1,0:T(8,128)(2,1)} %refs_5_.1), channel_id=1, source_target_pairs={{0,2},{1,3},{2,0},{3,1},{4,6},{5,7},{6,4},{7,5},{8,10},{9,11},{10,... | collective-permute-start | bytes 3145736 | tf_op jit(solution)/shard_map/ppermute | solution.py:582
  18.0 0.8 copy.13.refs_3_
  18.8 0.3 collective-permute-start.1
  19.1 0.5 collective-permute-start.8
  19.6 0.7 pad_add_fusion.refs_1_
  20.3 1.8 %collective-permute-start = (s32[3,32]{1,0:T(4,128)S(1)}, s32[3,32]{1,0:T(4,128)}, u32[]{:S(2)}, u32[]{:S(2)}) collective-permute-start(s32[3,32]{1,0:T(4,128)S(1)} %pad_add_fusion.refs_1_), channel_id=1, source_target_pairs={{0,2},{1,3},{2,0},{3,1},{4,6},{5,7},{6,4},{7,5},{8,10},{9,11},{10,... | collective-permute-start | bytes 1160 | tf_op jit(solution)/shard_map/ppermute | solution.py:582
  22.1 0.8 reshape.318.link_ref
  23.5 1.0 copy-done.5
  24.6 0.9 copy-done.6
  25.5 0.9 copy-done.8
  26.4 15.7 %shard_map.123 = (f32[2048,128]{1,0:T(8,128)S(1)}, bf16[1024,128]{1,0:T(8,128)(2,1)S(1)}) custom-call(s32[6144]{0:T(1024)S(1)} %reshape.318.link_ref, s32[1]{0:T(128)S(6)} %copy.16.live_ref, bf16[2048,128]{1,0:T(8,128)(2,1)S(1)} %copy-done.5, bf16[1024,128]{1,0:T(8,128)(2,1)S(1)} %copy-done.8, f32[36,1024]{1,0:T(8,128)S(1)} %copy-done.6), custom_call_target="tpu_custom_call" | custom-call | flops 4000000000 | bytes 3145728 | tf_op jit(solution)/shard_map/pallas_call | solution.py:416
  42.2 0.4 collective-permute-done.refs_1_
  42.6 0.5 collective-permute-start.5
  43.4 0.3 collective-permute-done.6.refs_2_
  43.7 0.2 collective-permute-start.3
  43.9 10.7 %shard_map.124.refs_7_ = f32[16,512,128]{2,1,0:T(8,128)S(1)} custom-call(f32[3,4]{1,0:T(4,128)S(1)} %copy-done.3, s32[3,32]{1,0:T(4,128)S(1)} %pad_add_fusion.refs_1_, s32[3,32]{1,0:T(4,128)S(1)} %collective-permute-done.6.refs_2_, bf16[32,3,128]{2,1,0:T(4,128)(2,1)S(1)} %copy.13.refs_3_, bf16[32,3,128]{2,1,0:T(4,128)(2,1)S(1)} %collective-permute-done.7.refs_4_, ...), custom_call_target="tpu_custom_call" | custom-call | flops 1073741824 | bytes 6291456 | tf_op jit(solution)/shard_map/pallas_call | solution.py:214
  54.7 11.2 %shard_map.125 = (f32[8,8,64,128]{3,2,1,0:T(8,128)S(1)}, bf16[8,8,64,128]{3,2,1,0:T(8,128)(2,1)S(1)}) custom-call(f32[3,4]{1,0:T(4,128)S(1)} %copy-done.3, s32[3,32]{1,0:T(4,128)} %collective-permute-done.refs_1_, s32[3,32]{1,0:T(4,128)S(1)} %collective-permute-done.3.refs_2_, bf16[32,3,128]{2,1,0:T(4,128)(2,1)S(1)} %collective-permute-done.1.refs_3_, ...), custom_call_target="tpu_custom_call" | custom-call | flops 1073741824 | bytes 6291456 | tf_op jit(solution)/shard_map/pallas_call | solution.py:214
  65.8 40.4 %shard_map.126 = (f32[2048,128]{1,0:T(8,128)S(1)}, f32[2,8,64,128]{3,2,1,0:T(8,128)S(1)}) custom-call(s32[1,1024]{1,0:T(1,128)S(1)} %reshape.319.row_ref, bf16[1024,128]{1,0:T(8,128)(2,1)S(1)} %get-tuple-element.18.back_ref, f32[8,8,64,128]{3,2,1,0:T(8,128)S(1)} %get-tuple-element.22.keep_ref, bf16[8,8,64,128]{3,2,1,0:T(8,128)(2,1)S(1)} %get-tuple-element.23.send_ref), custom_call_target="tpu_custom_call" | custom-call | flops 536870912 | bytes 3145728 | tf_op jit(solution)/shard_map/pallas_call | solution.py:529
  106.3 0.8 pad_maximum_fusion
  107.2 1.1 %add.73 = f32[2048,128]{1,0:T(8,128)} add(f32[2048,128]{1,0:T(8,128)S(1)} %get-tuple-element.15, f32[2048,128]{1,0:T(8,128)S(1)} %get-tuple-element.24) | non-fusion elementwise | flops 262144 | bytes 3145728 | tf_op jit(solution)/shard_map/add | solution.py:591
  (30 shorter events, 0.6 us)
Async XLA Ops:
  0.6 0.7 copy-start.1
  1.3 1.0 copy-start.4
  15.5 0.7 copy-start.7
  16.2 26.3 %collective-permute-start.2 = (bf16[32,128,128]{2,1,0:T(8,128)(2,1)}, bf16[32,128,128]{2,1,0:T(8,128)(2,1)S(1)}, u32[]{:S(2)}, u32[]{:S(2)}) collective-permute-start(bf16[32,128,128]{2,1,0:T(8,128)(2,1)} %refs_5_.1), channel_id=1, source_target_pairs={{0,2},{1,3},{2,0},{3,1},{4,6},{5,7},{6,4},{7,5},{8,10},{9,11},{10,... | collective-permute-start | bytes 3145736 | tf_op jit(solution)/shard_map/ppermute | solution.py:582
  18.8 23.8 %collective-permute-start.1 = (bf16[32,3,128]{2,1,0:T(4,128)(2,1)S(1)}, bf16[32,3,128]{2,1,0:T(4,128)(2,1)S(1)}, u32[]{:S(2)}, u32[]{:S(2)}) collective-permute-start(bf16[32,3,128]{2,1,0:T(4,128)(2,1)S(1)} %copy.13.refs_3_), channel_id=1, source_target_pairs={{0,2},{1,3},{2,0},{3,1},{4,6},{5,7},{6,4},{7,5},{8,10},{9,11},{10,... | collective-permute-start | bytes 73736 | tf_op jit(solution)/shard_map/ppermute | solution.py:582
  19.1 24.8 %collective-permute-start.7 = (bf16[32,3,128]{2,1,0:T(4,128)(2,1)S(1)}, bf16[32,3,128]{2,1,0:T(4,128)(2,1)S(1)}, u32[]{:S(2)}, u32[]{:S(2)}) collective-permute-start(bf16[32,3,128]{2,1,0:T(4,128)(2,1)S(1)} %copy.13.refs_3_), channel_id=1, source_target_pairs={{0,1},{1,0},{2,3},{3,2},{4,5},{5,4},{6,7},{7,6},{8,9},{9,8},{10,11... | collective-permute-start | bytes 73736 | tf_op jit(solution)/shard_map/ppermute | solution.py:66
  19.1 24.8 %collective-permute-start.8 = (bf16[32,128,128]{2,1,0:T(8,128)(2,1)}, bf16[32,128,128]{2,1,0:T(8,128)(2,1)}, u32[]{:S(2)}, u32[]{:S(2)}) collective-permute-start(bf16[32,128,128]{2,1,0:T(8,128)(2,1)} %refs_5_.1), channel_id=1, source_target_pairs={{0,1},{1,0},{2,3},{3,2},{4,5},{5,4},{6,7},{7,6},{8,9},{9,8},{10,11... | collective-permute-start | bytes 3145736 | tf_op jit(solution)/shard_map/ppermute | solution.py:66
  20.3 22.2 %collective-permute-start = (s32[3,32]{1,0:T(4,128)S(1)}, s32[3,32]{1,0:T(4,128)}, u32[]{:S(2)}, u32[]{:S(2)}) collective-permute-start(s32[3,32]{1,0:T(4,128)S(1)} %pad_add_fusion.refs_1_), channel_id=1, source_target_pairs={{0,2},{1,3},{2,0},{3,1},{4,6},{5,7},{6,4},{7,5},{8,10},{9,11},{10,... | collective-permute-start | bytes 1160 | tf_op jit(solution)/shard_map/ppermute | solution.py:582
  23.5 1.0 copy-start.5
  24.6 0.9 copy-start.6
  25.5 0.9 copy-start.8
  26.4 16.7 %copy-start.3 = (f32[3,4]{1,0:T(4,128)S(1)}, f32[3,4]{1,0:T(4,128)}, u32[]{:S(2)}) copy-start(f32[3,4]{1,0:T(4,128)} %refs_0_.3) | copy-start | bytes 148
  26.4 16.9 %copy-start.2 = (s32[32,32]{1,0:T(8,128)S(1)}, s32[32,32]{1,0:T(8,128)}, u32[]{:S(2)}) copy-start(s32[32,32]{1,0:T(8,128)} %list_ref.1) | copy-start | bytes 12292
  26.4 17.5 %copy-start = (bf16[32,128,128]{2,1,0:T(8,128)(2,1)S(1)}, bf16[32,128,128]{2,1,0:T(8,128)(2,1)}, u32[]{:S(2)}) copy-start(bf16[32,128,128]{2,1,0:T(8,128)(2,1)} %refs_5_.1) | copy-start | bytes 3145732
  42.5 1.2 %collective-permute-start.6 = (s32[3,32]{1,0:T(4,128)S(1)}, s32[3,32]{1,0:T(4,128)S(1)}, u32[]{:S(2)}, u32[]{:S(2)}) collective-permute-start(s32[3,32]{1,0:T(4,128)S(1)} %pad_add_fusion.refs_1_), channel_id=1, source_target_pairs={{0,1},{1,0},{2,3},{3,2},{4,5},{5,4},{6,7},{7,6},{8,9},{9,8},{10,11... | collective-permute-start | bytes 1160 | tf_op jit(solution)/shard_map/ppermute | solution.py:66
  42.6 12.1 %collective-permute-start.5 = (bf16[32,128,128]{2,1,0:T(8,128)(2,1)S(1)}, bf16[32,128,128]{2,1,0:T(8,128)(2,1)}, u32[]{:S(2)}, u32[]{:S(2)}) collective-permute-start(bf16[32,128,128]{2,1,0:T(8,128)(2,1)S(1)} %collective-permute-done.2.refs_5_), channel_id=1, source_target_pairs={{0,1},{1,0},{2,3},{3,2},{4,5},{5,4},{6,7},{7,6},{8,9},{9,8},{10,11... | collective-permute-start | bytes 3145736 | tf_op jit(solution)/shard_map/ppermute | solution.py:66
  43.4 11.3 %collective-permute-start.4 = (bf16[32,3,128]{2,1,0:T(4,128)(2,1)S(1)}, bf16[32,3,128]{2,1,0:T(4,128)(2,1)S(1)}, u32[]{:S(2)}, u32[]{:S(2)}) collective-permute-start(bf16[32,3,128]{2,1,0:T(4,128)(2,1)S(1)} %collective-permute-done.1.refs_3_), channel_id=1, source_target_pairs={{0,1},{1,0},{2,3},{3,2},{4,5},{5,4},{6,7},{7,6},{8,9},{9,8},{10,11... | collective-permute-start | bytes 73736 | tf_op jit(solution)/shard_map/ppermute | solution.py:66
  43.7 10.9 %collective-permute-start.3 = (s32[3,32]{1,0:T(4,128)}, s32[3,32]{1,0:T(4,128)S(1)}, u32[]{:S(2)}, u32[]{:S(2)}) collective-permute-start(s32[3,32]{1,0:T(4,128)} %collective-permute-done.refs_1_), channel_id=1, source_target_pairs={{0,1},{1,0},{2,3},{3,2},{4,5},{5,4},{6,7},{7,6},{8,9},{9,8},{10,11... | collective-permute-start | bytes 1160 | tf_op jit(solution)/shard_map/ppermute | solution.py:66

commit v3 on v2

--- a/solution.py
+++ b/solution.py
@@ -75,7 +75,7 @@
     total = lists * per_list
     height = units * SQUARE
     firsts = units * NODES
-    rows = PLANE + firsts
+    rows = PLANE + firsts + 8
     group = 16
     place_rows = 8
     half = slot_count // 2
@@ -163,24 +163,18 @@
             ]
             return jnp.concatenate(pieces, axis=0)
 
-        empty = jnp.zeros((block_size, columns), jnp.bfloat16)
         for which in range(lists):
-            def two(pair, carry):
-                index = which * per_list + 2 * pair
-                weights = jnp.concatenate([weights_of(index), weights_of(index + 1)], axis=1)
-                wide = jnp.concatenate(
-                    [
-                        jnp.concatenate([block_refs[which][2 * pair], empty], axis=1),
-                        jnp.concatenate([empty, block_refs[which][2 * pair + 1]], axis=1),
-                    ],
-                    axis=0,
+
+            def one(index, carry):
+                product = jnp.dot(
+                    weights_of(which * per_list + index),
+                    block_refs[which][index],
+                    preferred_element_type=jnp.float32,
                 )
-                product = jnp.dot(weights, wide, preferred_element_type=jnp.float32)
-                sum_ref[slot_of(which, 2 * pair)] += product[:, :columns]
-                sum_ref[slot_of(which, 2 * pair + 1)] += product[:, columns:]
+                sum_ref[slot_of(which, index)] += product
                 return carry
 
-            lax.fori_loop(0, per_list // 2, two, 0)
+            lax.fori_loop(0, per_list, one, 0, unroll=8)
 
         if last:
 
@@ -443,6 +437,7 @@
     steps = log2(lax.axis_size("dom"))
     sizes = [half >> k for k in range(steps)]
     fold_step = 256
+    lag = 2
 
     def kernel(row_ref, back_ref, keep_ref, send_ref, fold_ref, out_ref, *scratch):
         land_ref = scratch[0]
@@ -488,11 +483,9 @@
 
             lax.fori_loop(0, owned_rows // fold_step, fold, 0)
 
-        for turn in range(units + steps - 1):
-            if turn == units:
-                fold_all()
-            for k in range(steps):
-                unit = turn - k
+        for turn in range(units + lag * (steps - 1)):
+            for k in reversed(range(steps)):
+                unit = turn - lag * k
                 if not 0 <= unit < units:
                     continue
                 copy(k, unit).wait_recv()
@@ -511,6 +504,8 @@
                         out_ref[parent, unit] = keeps[k][unit, parent] + got[k][
                             unit, parent
                         ].astype(jnp.float32)
+            if turn == units - 1 + lag * (steps - 2):
+                fold_all()
         whole.wait_send()
         for k in range(steps):
             for unit in range(units):

time: 109 us -> 98.5 us (0.904)
  Pallas kernels: 91.1 us -> 80.7 us
    pallas_call x2, Pallas kernels: 21.9 us -> 12.8 us  [block_sums(): pl.pallas_call(kernel, out_shape=out_shape, in_specs=[SMEM] * (1 + lists)...]
    pallas_call x1, Pallas kernels: 40.4 us -> 39.1 us  [return_and_reduce(): pl.pallas_call(kernel, out_shape=[jax.ShapeDtypeStruct((owned_rows, colum...]
  transfers between devices with their start and end apart: 9 -> 9, of which waited for: 2 -> 2; matrix products, arithmetic and copies ran while one was open for 2% -> 3% of each run, Pallas kernels for 24% -> 22%
where the time goes in v3:
time: 98.5 us; the launch traced here: 98 us
  Pallas kernels  80.7 us (82%)
  local copies, waits for them, and re-layouts  6.97 us (7%)
  starting transfers between devices  5.17 us (5%)
  other arithmetic  2.99 us (3%)
  between operations  1.42 us (1%)
    pallas_call x1, Pallas kernels, return_and_reduce(): pl.pallas_call(kernel, out_shape=[jax.ShapeDtypeStruct((owned_rows, colum...  39.1 us
    pallas_call x1, Pallas kernels, element_sums(): pl.pallas_call(kernel, out_shape=[jax.ShapeDtypeStruct((owned_rows, colum...  15.7 us
    pallas_call x1, Pallas kernels, halo_rows(): pl.pallas_call(kernel, out_shape=jax.ShapeDtypeStruct((partitions * width...  13.1 us
    pallas_call x2, Pallas kernels, block_sums(): pl.pallas_call(kernel, out_shape=out_shape, in_specs=[SMEM] * (1 + lists)...  12.8 us
    unnamed x19, local copies, waits for them, and re-layouts  6.12 us
    ppermute x3, starting transfers between devices, shards(): lax.ppermute(value, 'dir', xor_pairs(dir_count, dir_bits - 1))  3.89 us
  transfers between devices with their start and end apart: 9, of which 2 were waited for; matrix products, arithmetic and copies ran while one was open for 3% of the time, Pallas kernels for 22%

profile of v3, /device:TPU:0, one launch (start us, length us, event | category | flops | bytes accessed | tf_op | source)
XLA Modules:
  0.0 98.0 jit_solution(10639279816439947961)
XLA Ops:
  0.6 0.7 copy-done.1
  1.4 1.0 %copy-done.4 = bf16[2048,128]{1,0:T(8,128)(2,1)S(1)} copy-done((bf16[2048,128]{1,0:T(8,128)(2,1)S(1)}, bf16[2048,128]{1,0:T(8,128)(2,1)}, u32[]{:S(2)}) %copy-start.4) | copy-done | bytes 524312
  2.4 13.1 %shard_map.122.halo_ref = bf16[1024,128]{1,0:T(8,128)(2,1)S(1)} custom-call(s32[32,32]{1,0:T(8,128)S(1)} %copy-done.1, bf16[2048,128]{1,0:T(8,128)(2,1)S(1)} %copy-done.4), custom_call_target="tpu_custom_call" | custom-call | flops 1000000000 | bytes 524288 | tf_op jit(solution)/shard_map/pallas_call | solution.py:315
  15.5 0.7 copy-done.7
  16.2 1.8 %collective-permute-start.2 = (bf16[32,128,128]{2,1,0:T(8,128)(2,1)}, bf16[32,128,128]{2,1,0:T(8,128)(2,1)S(1)}, u32[]{:S(2)}, u32[]{:S(2)}) collective-permute-start(bf16[32,128,128]{2,1,0:T(8,128)(2,1)} %refs_5_.1), channel_id=1, source_target_pairs={{0,2},{1,3},{2,0},{3,1},{4,6},{5,7},{6,4},{7,5},{8,10},{9,11},{10,... | collective-permute-start | bytes 3145736 | tf_op jit(solution)/shard_map/ppermute | solution.py:577
  18.0 0.8 copy.13.refs_3_
  18.8 0.3 collective-permute-start.1
  19.1 0.5 collective-permute-start.8
  19.6 0.7 pad_add_fusion.refs_1_
  20.3 1.8 %collective-permute-start = (s32[3,32]{1,0:T(4,128)S(1)}, s32[3,32]{1,0:T(4,128)}, u32[]{:S(2)}, u32[]{:S(2)}) collective-permute-start(s32[3,32]{1,0:T(4,128)S(1)} %pad_add_fusion.refs_1_), channel_id=1, source_target_pairs={{0,2},{1,3},{2,0},{3,1},{4,6},{5,7},{6,4},{7,5},{8,10},{9,11},{10,... | collective-permute-start | bytes 1160 | tf_op jit(solution)/shard_map/ppermute | solution.py:577
  22.1 0.8 reshape.318.link_ref
  23.5 1.0 %copy-done.5 = bf16[2048,128]{1,0:T(8,128)(2,1)S(1)} copy-done((bf16[2048,128]{1,0:T(8,128)(2,1)S(1)}, bf16[2048,128]{1,0:T(8,128)(2,1)}, u32[]{:S(2)}) %copy-start.5) | copy-done | bytes 524312
  24.6 0.9 copy-done.6
  25.5 0.9 copy-done.8
  26.4 15.7 %shard_map.123 = (f32[2048,128]{1,0:T(8,128)S(1)}, bf16[1024,128]{1,0:T(8,128)(2,1)S(1)}) custom-call(s32[6144]{0:T(1024)S(1)} %reshape.318.link_ref, s32[1]{0:T(128)S(6)} %copy.16.live_ref, bf16[2048,128]{1,0:T(8,128)(2,1)S(1)} %copy-done.5, bf16[1024,128]{1,0:T(8,128)(2,1)S(1)} %copy-done.8, f32[36,1024]{1,0:T(8,128)S(1)} %copy-done.6), custom_call_target="tpu_custom_call" | custom-call | flops 4000000000 | bytes 3145728 | tf_op jit(solution)/shard_map/pallas_call | solution.py:410
  42.1 0.4 collective-permute-done.refs_1_
  42.6 0.5 collective-permute-start.5
  43.4 0.3 collective-permute-done.6.refs_2_
  43.7 0.2 collective-permute-start.3
  43.9 6.3 %shard_map.124.refs_7_ = f32[16,512,128]{2,1,0:T(8,128)S(1)} custom-call(f32[3,4]{1,0:T(4,128)S(1)} %copy-done.3, s32[3,32]{1,0:T(4,128)S(1)} %pad_add_fusion.refs_1_, s32[3,32]{1,0:T(4,128)S(1)} %collective-permute-done.6.refs_2_, bf16[32,3,128]{2,1,0:T(4,128)(2,1)S(1)} %copy.13.refs_3_, bf16[32,3,128]{2,1,0:T(4,128)(2,1)S(1)} %collective-permute-done.7.refs_4_, ...), custom_call_target="tpu_custom_call" | custom-call | flops 1073741824 | bytes 6291456 | tf_op jit(solution)/shard_map/pallas_call | solution.py:208
  50.3 6.5 %shard_map.125 = (f32[8,8,64,128]{3,2,1,0:T(8,128)S(1)}, bf16[8,8,64,128]{3,2,1,0:T(8,128)(2,1)S(1)}) custom-call(f32[3,4]{1,0:T(4,128)S(1)} %copy-done.3, s32[3,32]{1,0:T(4,128)} %collective-permute-done.refs_1_, s32[3,32]{1,0:T(4,128)S(1)} %collective-permute-done.3.refs_2_, bf16[32,3,128]{2,1,0:T(4,128)(2,1)S(1)} %collective-permute-done.1.refs_3_, ...), custom_call_target="tpu_custom_call" | custom-call | flops 1073741824 | bytes 6291456 | tf_op jit(solution)/shard_map/pallas_call | solution.py:208
  56.8 39.1 %shard_map.126 = (f32[2048,128]{1,0:T(8,128)S(1)}, f32[2,8,64,128]{3,2,1,0:T(8,128)S(1)}) custom-call(s32[1,1024]{1,0:T(1,128)S(1)} %reshape.319.row_ref, bf16[1024,128]{1,0:T(8,128)(2,1)S(1)} %get-tuple-element.18.back_ref, f32[8,8,64,128]{3,2,1,0:T(8,128)S(1)} %get-tuple-element.22.keep_ref, bf16[8,8,64,128]{3,2,1,0:T(8,128)(2,1)S(1)} %get-tuple-element.23.send_ref), custom_call_target="tpu_custom_call" | custom-call | flops 536870912 | bytes 3145728 | tf_op jit(solution)/shard_map/pallas_call | solution.py:524
  96.0 0.8 pad_maximum_fusion
  96.8 1.1 %add.73 = f32[2048,128]{1,0:T(8,128)} add(f32[2048,128]{1,0:T(8,128)S(1)} %get-tuple-element.15, f32[2048,128]{1,0:T(8,128)S(1)} %get-tuple-element.24) | non-fusion elementwise | flops 262144 | bytes 3145728 | tf_op jit(solution)/shard_map/add | solution.py:586
  (30 shorter events, 0.6 us)
Async XLA Ops:
  0.6 0.7 copy-start.1
  1.3 1.0 %copy-start.4 = (bf16[2048,128]{1,0:T(8,128)(2,1)S(1)}, bf16[2048,128]{1,0:T(8,128)(2,1)}, u32[]{:S(2)}) copy-start(bf16[2048,128]{1,0:T(8,128)(2,1)} %x_ref.3) | copy-start | bytes 1572868
  15.5 0.7 copy-start.7
  16.2 26.3 %collective-permute-start.2 = (bf16[32,128,128]{2,1,0:T(8,128)(2,1)}, bf16[32,128,128]{2,1,0:T(8,128)(2,1)S(1)}, u32[]{:S(2)}, u32[]{:S(2)}) collective-permute-start(bf16[32,128,128]{2,1,0:T(8,128)(2,1)} %refs_5_.1), channel_id=1, source_target_pairs={{0,2},{1,3},{2,0},{3,1},{4,6},{5,7},{6,4},{7,5},{8,10},{9,11},{10,... | collective-permute-start | bytes 3145736 | tf_op jit(solution)/shard_map/ppermute | solution.py:577
  18.8 23.8 %collective-permute-start.1 = (bf16[32,3,128]{2,1,0:T(4,128)(2,1)S(1)}, bf16[32,3,128]{2,1,0:T(4,128)(2,1)S(1)}, u32[]{:S(2)}, u32[]{:S(2)}) collective-permute-start(bf16[32,3,128]{2,1,0:T(4,128)(2,1)S(1)} %copy.13.refs_3_), channel_id=1, source_target_pairs={{0,2},{1,3},{2,0},{3,1},{4,6},{5,7},{6,4},{7,5},{8,10},{9,11},{10,... | collective-permute-start | bytes 73736 | tf_op jit(solution)/shard_map/ppermute | solution.py:577
  19.1 24.8 %collective-permute-start.7 = (bf16[32,3,128]{2,1,0:T(4,128)(2,1)S(1)}, bf16[32,3,128]{2,1,0:T(4,128)(2,1)S(1)}, u32[]{:S(2)}, u32[]{:S(2)}) collective-permute-start(bf16[32,3,128]{2,1,0:T(4,128)(2,1)S(1)} %copy.13.refs_3_), channel_id=1, source_target_pairs={{0,1},{1,0},{2,3},{3,2},{4,5},{5,4},{6,7},{7,6},{8,9},{9,8},{10,11... | collective-permute-start | bytes 73736 | tf_op jit(solution)/shard_map/ppermute | solution.py:66
  19.1 24.8 %collective-permute-start.8 = (bf16[32,128,128]{2,1,0:T(8,128)(2,1)}, bf16[32,128,128]{2,1,0:T(8,128)(2,1)}, u32[]{:S(2)}, u32[]{:S(2)}) collective-permute-start(bf16[32,128,128]{2,1,0:T(8,128)(2,1)} %refs_5_.1), channel_id=1, source_target_pairs={{0,1},{1,0},{2,3},{3,2},{4,5},{5,4},{6,7},{7,6},{8,9},{9,8},{10,11... | collective-permute-start | bytes 3145736 | tf_op jit(solution)/shard_map/ppermute | solution.py:66
  20.3 22.2 %collective-permute-start = (s32[3,32]{1,0:T(4,128)S(1)}, s32[3,32]{1,0:T(4,128)}, u32[]{:S(2)}, u32[]{:S(2)}) collective-permute-start(s32[3,32]{1,0:T(4,128)S(1)} %pad_add_fusion.refs_1_), channel_id=1, source_target_pairs={{0,2},{1,3},{2,0},{3,1},{4,6},{5,7},{6,4},{7,5},{8,10},{9,11},{10,... | collective-permute-start | bytes 1160 | tf_op jit(solution)/shard_map/ppermute | solution.py:577
  23.5 1.0 %copy-start.5 = (bf16[2048,128]{1,0:T(8,128)(2,1)S(1)}, bf16[2048,128]{1,0:T(8,128)(2,1)}, u32[]{:S(2)}) copy-start(bf16[2048,128]{1,0:T(8,128)(2,1)} %x_ref.3) | copy-start | bytes 1572868
  24.6 0.9 copy-start.6
  25.5 0.9 copy-start.8
  26.4 16.7 %copy-start.3 = (f32[3,4]{1,0:T(4,128)S(1)}, f32[3,4]{1,0:T(4,128)}, u32[]{:S(2)}) copy-start(f32[3,4]{1,0:T(4,128)} %refs_0_.3) | copy-start | bytes 148
  26.4 16.9 %copy-start.2 = (s32[32,32]{1,0:T(8,128)S(1)}, s32[32,32]{1,0:T(8,128)}, u32[]{:S(2)}) copy-start(s32[32,32]{1,0:T(8,128)} %list_ref.1) | copy-start | bytes 12292
  26.4 17.5 %copy-start = (bf16[32,128,128]{2,1,0:T(8,128)(2,1)S(1)}, bf16[32,128,128]{2,1,0:T(8,128)(2,1)}, u32[]{:S(2)}) copy-start(bf16[32,128,128]{2,1,0:T(8,128)(2,1)} %refs_5_.1) | copy-start | bytes 3145732
  42.5 1.2 %collective-permute-start.6 = (s32[3,32]{1,0:T(4,128)S(1)}, s32[3,32]{1,0:T(4,128)S(1)}, u32[]{:S(2)}, u32[]{:S(2)}) collective-permute-start(s32[3,32]{1,0:T(4,128)S(1)} %pad_add_fusion.refs_1_), channel_id=1, source_target_pairs={{0,1},{1,0},{2,3},{3,2},{4,5},{5,4},{6,7},{7,6},{8,9},{9,8},{10,11... | collective-permute-start | bytes 1160 | tf_op jit(solution)/shard_map/ppermute | solution.py:66
  42.6 7.7 %collective-permute-start.5 = (bf16[32,128,128]{2,1,0:T(8,128)(2,1)S(1)}, bf16[32,128,128]{2,1,0:T(8,128)(2,1)}, u32[]{:S(2)}, u32[]{:S(2)}) collective-permute-start(bf16[32,128,128]{2,1,0:T(8,128)(2,1)S(1)} %collective-permute-done.2.refs_5_), channel_id=1, source_target_pairs={{0,1},{1,0},{2,3},{3,2},{4,5},{5,4},{6,7},{7,6},{8,9},{9,8},{10,11... | collective-permute-start | bytes 3145736 | tf_op jit(solution)/shard_map/ppermute | solution.py:66
  43.4 6.9 %collective-permute-start.4 = (bf16[32,3,128]{2,1,0:T(4,128)(2,1)S(1)}, bf16[32,3,128]{2,1,0:T(4,128)(2,1)S(1)}, u32[]{:S(2)}, u32[]{:S(2)}) collective-permute-start(bf16[32,3,128]{2,1,0:T(4,128)(2,1)S(1)} %collective-permute-done.1.refs_3_), channel_id=1, source_target_pairs={{0,1},{1,0},{2,3},{3,2},{4,5},{5,4},{6,7},{7,6},{8,9},{9,8},{10,11... | collective-permute-start | bytes 73736 | tf_op jit(solution)/shard_map/ppermute | solution.py:66
  43.7 6.5 %collective-permute-start.3 = (s32[3,32]{1,0:T(4,128)}, s32[3,32]{1,0:T(4,128)S(1)}, u32[]{:S(2)}, u32[]{:S(2)}) collective-permute-start(s32[3,32]{1,0:T(4,128)} %collective-permute-done.refs_1_), channel_id=1, source_target_pairs={{0,1},{1,0},{2,3},{3,2},{4,5},{5,4},{6,7},{7,6},{8,9},{9,8},{10,11... | collective-permute-start | bytes 1160 | tf_op jit(solution)/shard_map/ppermute | solution.py:66

commit v4 on v3

--- a/solution.py
+++ b/solution.py
@@ -59,6 +59,10 @@
     return bits
 
 
+def turned_units(units):
+    return units // 4
+
+
 def spread(value, axis, bits):
     held = [value]
     count = lax.axis_size(axis)
@@ -178,12 +182,20 @@
 
         if last:
 
+            def turned_back(slot):
+                owner = slot // parents
+                owner = owner // 2 + owner % 2 * (half // parents)
+                return owner * parents + slot % parents
+
             def finish(slot, carry):
                 for unit in range(units):
                     span = pl.ds(unit * SQUARE, SQUARE)
-                    keep_ref[unit, slot] = sum_ref[slot, span, :] + before_ref[slot, span, :]
+                    kept, sent = slot, half + slot
+                    if unit < turned_units(units):
+                        kept, sent = turned_back(kept), turned_back(sent)
+                    keep_ref[unit, slot] = sum_ref[kept, span, :] + before_ref[kept, span, :]
                     send_ref[unit, slot] = (
-                        sum_ref[half + slot, span, :] + before_ref[half + slot, span, :]
+                        sum_ref[sent, span, :] + before_ref[sent, span, :]
                     ).astype(jnp.bfloat16)
                 return carry
 
@@ -437,7 +449,8 @@
     steps = log2(lax.axis_size("dom"))
     sizes = [half >> k for k in range(steps)]
     fold_step = 256
-    lag = 2
+    lag = 3
+    turned = turned_units(units)
 
     def kernel(row_ref, back_ref, keep_ref, send_ref, fold_ref, out_ref, *scratch):
         land_ref = scratch[0]
@@ -452,7 +465,7 @@
         land_ref[own, :] = jnp.zeros((width, columns), jnp.bfloat16)
         pl.semaphore_wait(barrier, others)
         def copy(k, unit):
-            bit = 1 << k
+            bit = 1 << ((k + 1) % steps if unit < turned else k)
             partner = dom + bit * (1 - 2 * ((dom // bit) % 2))
             return pltpu.make_async_remote_copy(
                 src_ref=sends[k].at[unit],
@@ -483,28 +496,32 @@
 
             lax.fori_loop(0, owned_rows // fold_step, fold, 0)
 
+        def step(k, unit):
+            copy(k, unit).wait_recv()
+            if k < steps - 1:
+                low = sizes[k + 1]
+                upper, lower = pl.ds(low, low), pl.ds(0, low)
+                sends[k + 1][unit] = (
+                    keeps[k][unit, upper] + got[k][unit, upper].astype(jnp.float32)
+                ).astype(jnp.bfloat16)
+                copy(k + 1, unit).start()
+                keeps[k + 1][unit] = keeps[k][unit, lower] + got[k][unit, lower].astype(
+                    jnp.float32
+                )
+            else:
+                for parent in range(parents):
+                    out_ref[parent, unit] = keeps[k][unit, parent] + got[k][unit, parent].astype(
+                        jnp.float32
+                    )
+
         for turn in range(units + lag * (steps - 1)):
             for k in reversed(range(steps)):
                 unit = turn - lag * k
-                if not 0 <= unit < units:
-                    continue
-                copy(k, unit).wait_recv()
-                if k < steps - 1:
-                    low = sizes[k + 1]
-                    upper, lower = pl.ds(low, low), pl.ds(0, low)
-                    sends[k + 1][unit] = (
-                        keeps[k][unit, upper] + got[k][unit, upper].astype(jnp.float32)
-                    ).astype(jnp.bfloat16)
-                    copy(k + 1, unit).start()
-                    keeps[k + 1][unit] = keeps[k][unit, lower] + got[k][unit, lower].astype(
-                        jnp.float32
-                    )
-                else:
-                    for parent in range(parents):
-                        out_ref[parent, unit] = keeps[k][unit, parent] + got[k][
-                            unit, parent
-                        ].astype(jnp.float32)
+                if 0 <= unit < units and not (k == steps - 1 and unit < turned):
+                    step(k, unit)
             if turn == units - 1 + lag * (steps - 2):
+                for unit in range(turned):
+                    step(steps - 1, unit)
                 fold_all()
         whole.wait_send()
         for k in range(steps):

time: 98.5 us -> 95.9 us (0.974)
  Pallas kernels: 80.7 us -> 78.2 us
    pallas_call x1, Pallas kernels: 39.1 us -> 36.5 us  [return_and_reduce(): pl.pallas_call(kernel, out_shape=[jax.ShapeDtypeStruct((owned_rows, colum...]
  transfers between devices with their start and end apart: 9 -> 9, of which waited for: 2 -> 2; matrix products, arithmetic and copies ran while one was open for 3% -> 3% of each run, Pallas kernels for 22% -> 23%
where the time goes in v4:
time: 95.9 us; the launch traced here: 95.4 us
  Pallas kernels  78.2 us (82%)
  local copies, waits for them, and re-layouts  6.97 us (7%)
  starting transfers between devices  5.17 us (5%)
  other arithmetic  2.99 us (3%)
  between operations  1.42 us (1%)
    pallas_call x1, Pallas kernels, return_and_reduce(): pl.pallas_call(kernel, out_shape=[jax.ShapeDtypeStruct((owned_rows, colum...  36.5 us
    pallas_call x1, Pallas kernels, element_sums(): pl.pallas_call(kernel, out_shape=[jax.ShapeDtypeStruct((owned_rows, colum...  15.7 us
    pallas_call x1, Pallas kernels, halo_rows(): pl.pallas_call(kernel, out_shape=jax.ShapeDtypeStruct((partitions * width...  13.1 us
    pallas_call x2, Pallas kernels, block_sums(): pl.pallas_call(kernel, out_shape=out_shape, in_specs=[SMEM] * (1 + lists)...  12.9 us
    unnamed x19, local copies, waits for them, and re-layouts  6.12 us
    ppermute x3, starting transfers between devices, shards(): lax.ppermute(value, 'dir', xor_pairs(dir_count, dir_bits - 1))  3.89 us
  transfers between devices with their start and end apart: 9, of which 2 were waited for; matrix products, arithmetic and copies ran while one was open for 3% of the time, Pallas kernels for 23%

profile of v4, /device:TPU:0, one launch (start us, length us, event | category | flops | bytes accessed | tf_op | source)
XLA Modules:
  0.0 95.4 jit_solution(5945391128173658614)
XLA Ops:
  0.6 0.7 copy-done.1
  1.4 1.0 %copy-done.4 = bf16[2048,128]{1,0:T(8,128)(2,1)S(1)} copy-done((bf16[2048,128]{1,0:T(8,128)(2,1)S(1)}, bf16[2048,128]{1,0:T(8,128)(2,1)}, u32[]{:S(2)}) %copy-start.4) | copy-done | bytes 524312
  2.4 13.1 %shard_map.122.halo_ref = bf16[1024,128]{1,0:T(8,128)(2,1)S(1)} custom-call(s32[32,32]{1,0:T(8,128)S(1)} %copy-done.1, bf16[2048,128]{1,0:T(8,128)(2,1)S(1)} %copy-done.4), custom_call_target="tpu_custom_call" | custom-call | flops 1000000000 | bytes 524288 | tf_op jit(solution)/shard_map/pallas_call | solution.py:327
  15.5 0.7 copy-done.7
  16.2 1.8 %collective-permute-start.2 = (bf16[32,128,128]{2,1,0:T(8,128)(2,1)}, bf16[32,128,128]{2,1,0:T(8,128)(2,1)S(1)}, u32[]{:S(2)}, u32[]{:S(2)}) collective-permute-start(bf16[32,128,128]{2,1,0:T(8,128)(2,1)} %refs_5_.1), channel_id=1, source_target_pairs={{0,2},{1,3},{2,0},{3,1},{4,6},{5,7},{6,4},{7,5},{8,10},{9,11},{10,... | collective-permute-start | bytes 3145736 | tf_op jit(solution)/shard_map/ppermute | solution.py:594
  18.0 0.8 copy.13.refs_3_
  18.8 0.3 collective-permute-start.1
  19.1 0.5 collective-permute-start.8
  19.6 0.7 pad_add_fusion.refs_1_
  20.3 1.8 %collective-permute-start = (s32[3,32]{1,0:T(4,128)S(1)}, s32[3,32]{1,0:T(4,128)}, u32[]{:S(2)}, u32[]{:S(2)}) collective-permute-start(s32[3,32]{1,0:T(4,128)S(1)} %pad_add_fusion.refs_1_), channel_id=1, source_target_pairs={{0,2},{1,3},{2,0},{3,1},{4,6},{5,7},{6,4},{7,5},{8,10},{9,11},{10,... | collective-permute-start | bytes 1160 | tf_op jit(solution)/shard_map/ppermute | solution.py:594
  22.1 0.8 reshape.318.link_ref
  23.5 1.0 %copy-done.5 = bf16[2048,128]{1,0:T(8,128)(2,1)S(1)} copy-done((bf16[2048,128]{1,0:T(8,128)(2,1)S(1)}, bf16[2048,128]{1,0:T(8,128)(2,1)}, u32[]{:S(2)}) %copy-start.5) | copy-done | bytes 524312
  24.6 0.9 copy-done.6
  25.5 0.9 copy-done.8
  26.4 15.7 %shard_map.123 = (f32[2048,128]{1,0:T(8,128)S(1)}, bf16[1024,128]{1,0:T(8,128)(2,1)S(1)}) custom-call(s32[6144]{0:T(1024)S(1)} %reshape.318.link_ref, s32[1]{0:T(128)S(6)} %copy.16.live_ref, bf16[2048,128]{1,0:T(8,128)(2,1)S(1)} %copy-done.5, bf16[1024,128]{1,0:T(8,128)(2,1)S(1)} %copy-done.8, f32[36,1024]{1,0:T(8,128)S(1)} %copy-done.6), custom_call_target="tpu_custom_call" | custom-call | flops 4000000000 | bytes 3145728 | tf_op jit(solution)/shard_map/pallas_call | solution.py:422
  42.1 0.4 collective-permute-done.refs_1_
  42.6 0.5 collective-permute-start.5
  43.4 0.3 collective-permute-done.6.refs_2_
  43.7 0.2 collective-permute-start.3
  43.9 6.3 %shard_map.124.refs_7_ = f32[16,512,128]{2,1,0:T(8,128)S(1)} custom-call(f32[3,4]{1,0:T(4,128)S(1)} %copy-done.3, s32[3,32]{1,0:T(4,128)S(1)} %pad_add_fusion.refs_1_, s32[3,32]{1,0:T(4,128)S(1)} %collective-permute-done.6.refs_2_, bf16[32,3,128]{2,1,0:T(4,128)(2,1)S(1)} %copy.13.refs_3_, bf16[32,3,128]{2,1,0:T(4,128)(2,1)S(1)} %collective-permute-done.7.refs_4_, ...), custom_call_target="tpu_custom_call" | custom-call | flops 1073741824 | bytes 6291456 | tf_op jit(solution)/shard_map/pallas_call | solution.py:220
  50.3 6.6 %shard_map.125 = (f32[8,8,64,128]{3,2,1,0:T(8,128)S(1)}, bf16[8,8,64,128]{3,2,1,0:T(8,128)(2,1)S(1)}) custom-call(f32[3,4]{1,0:T(4,128)S(1)} %copy-done.3, s32[3,32]{1,0:T(4,128)} %collective-permute-done.refs_1_, s32[3,32]{1,0:T(4,128)S(1)} %collective-permute-done.3.refs_2_, bf16[32,3,128]{2,1,0:T(4,128)(2,1)S(1)} %collective-permute-done.1.refs_3_, ...), custom_call_target="tpu_custom_call" | custom-call | flops 1073741824 | bytes 6291456 | tf_op jit(solution)/shard_map/pallas_call | solution.py:220
  56.8 36.5 %shard_map.126 = (f32[2048,128]{1,0:T(8,128)S(1)}, f32[2,8,64,128]{3,2,1,0:T(8,128)S(1)}) custom-call(s32[1,1024]{1,0:T(1,128)S(1)} %reshape.319.row_ref, bf16[1024,128]{1,0:T(8,128)(2,1)S(1)} %get-tuple-element.18.back_ref, f32[8,8,64,128]{3,2,1,0:T(8,128)S(1)} %get-tuple-element.22.keep_ref, bf16[8,8,64,128]{3,2,1,0:T(8,128)(2,1)S(1)} %get-tuple-element.23.send_ref), custom_call_target="tpu_custom_call" | custom-call | flops 536870912 | bytes 3145728 | tf_op jit(solution)/shard_map/pallas_call | solution.py:541
  93.5 0.8 pad_maximum_fusion
  94.3 1.1 %add.73 = f32[2048,128]{1,0:T(8,128)} add(f32[2048,128]{1,0:T(8,128)S(1)} %get-tuple-element.15, f32[2048,128]{1,0:T(8,128)S(1)} %get-tuple-element.24) | non-fusion elementwise | flops 262144 | bytes 3145728 | tf_op jit(solution)/shard_map/add | solution.py:603
  (30 shorter events, 0.6 us)
Async XLA Ops:
  0.6 0.7 copy-start.1
  1.3 1.0 %copy-start.4 = (bf16[2048,128]{1,0:T(8,128)(2,1)S(1)}, bf16[2048,128]{1,0:T(8,128)(2,1)}, u32[]{:S(2)}) copy-start(bf16[2048,128]{1,0:T(8,128)(2,1)} %x_ref.3) | copy-start | bytes 1572868
  15.5 0.7 copy-start.7
  16.2 26.3 %collective-permute-start.2 = (bf16[32,128,128]{2,1,0:T(8,128)(2,1)}, bf16[32,128,128]{2,1,0:T(8,128)(2,1)S(1)}, u32[]{:S(2)}, u32[]{:S(2)}) collective-permute-start(bf16[32,128,128]{2,1,0:T(8,128)(2,1)} %refs_5_.1), channel_id=1, source_target_pairs={{0,2},{1,3},{2,0},{3,1},{4,6},{5,7},{6,4},{7,5},{8,10},{9,11},{10,... | collective-permute-start | bytes 3145736 | tf_op jit(solution)/shard_map/ppermute | solution.py:594
  18.8 23.8 %collective-permute-start.1 = (bf16[32,3,128]{2,1,0:T(4,128)(2,1)S(1)}, bf16[32,3,128]{2,1,0:T(4,128)(2,1)S(1)}, u32[]{:S(2)}, u32[]{:S(2)}) collective-permute-start(bf16[32,3,128]{2,1,0:T(4,128)(2,1)S(1)} %copy.13.refs_3_), channel_id=1, source_target_pairs={{0,2},{1,3},{2,0},{3,1},{4,6},{5,7},{6,4},{7,5},{8,10},{9,11},{10,... | collective-permute-start | bytes 73736 | tf_op jit(solution)/shard_map/ppermute | solution.py:594
  19.1 24.8 %collective-permute-start.7 = (bf16[32,3,128]{2,1,0:T(4,128)(2,1)S(1)}, bf16[32,3,128]{2,1,0:T(4,128)(2,1)S(1)}, u32[]{:S(2)}, u32[]{:S(2)}) collective-permute-start(bf16[32,3,128]{2,1,0:T(4,128)(2,1)S(1)} %copy.13.refs_3_), channel_id=1, source_target_pairs={{0,1},{1,0},{2,3},{3,2},{4,5},{5,4},{6,7},{7,6},{8,9},{9,8},{10,11... | collective-permute-start | bytes 73736 | tf_op jit(solution)/shard_map/ppermute | solution.py:70
  19.1 24.8 %collective-permute-start.8 = (bf16[32,128,128]{2,1,0:T(8,128)(2,1)}, bf16[32,128,128]{2,1,0:T(8,128)(2,1)}, u32[]{:S(2)}, u32[]{:S(2)}) collective-permute-start(bf16[32,128,128]{2,1,0:T(8,128)(2,1)} %refs_5_.1), channel_id=1, source_target_pairs={{0,1},{1,0},{2,3},{3,2},{4,5},{5,4},{6,7},{7,6},{8,9},{9,8},{10,11... | collective-permute-start | bytes 3145736 | tf_op jit(solution)/shard_map/ppermute | solution.py:70
  20.3 22.2 %collective-permute-start = (s32[3,32]{1,0:T(4,128)S(1)}, s32[3,32]{1,0:T(4,128)}, u32[]{:S(2)}, u32[]{:S(2)}) collective-permute-start(s32[3,32]{1,0:T(4,128)S(1)} %pad_add_fusion.refs_1_), channel_id=1, source_target_pairs={{0,2},{1,3},{2,0},{3,1},{4,6},{5,7},{6,4},{7,5},{8,10},{9,11},{10,... | collective-permute-start | bytes 1160 | tf_op jit(solution)/shard_map/ppermute | solution.py:594
  23.5 1.0 %copy-start.5 = (bf16[2048,128]{1,0:T(8,128)(2,1)S(1)}, bf16[2048,128]{1,0:T(8,128)(2,1)}, u32[]{:S(2)}) copy-start(bf16[2048,128]{1,0:T(8,128)(2,1)} %x_ref.3) | copy-start | bytes 1572868
  24.6 0.9 copy-start.6
  25.5 0.9 copy-start.8
  26.4 16.7 %copy-start.3 = (f32[3,4]{1,0:T(4,128)S(1)}, f32[3,4]{1,0:T(4,128)}, u32[]{:S(2)}) copy-start(f32[3,4]{1,0:T(4,128)} %refs_0_.3) | copy-start | bytes 148
  26.4 16.9 %copy-start.2 = (s32[32,32]{1,0:T(8,128)S(1)}, s32[32,32]{1,0:T(8,128)}, u32[]{:S(2)}) copy-start(s32[32,32]{1,0:T(8,128)} %list_ref.1) | copy-start | bytes 12292
  26.4 17.5 %copy-start = (bf16[32,128,128]{2,1,0:T(8,128)(2,1)S(1)}, bf16[32,128,128]{2,1,0:T(8,128)(2,1)}, u32[]{:S(2)}) copy-start(bf16[32,128,128]{2,1,0:T(8,128)(2,1)} %refs_5_.1) | copy-start | bytes 3145732
  42.5 1.2 %collective-permute-start.6 = (s32[3,32]{1,0:T(4,128)S(1)}, s32[3,32]{1,0:T(4,128)S(1)}, u32[]{:S(2)}, u32[]{:S(2)}) collective-permute-start(s32[3,32]{1,0:T(4,128)S(1)} %pad_add_fusion.refs_1_), channel_id=1, source_target_pairs={{0,1},{1,0},{2,3},{3,2},{4,5},{5,4},{6,7},{7,6},{8,9},{9,8},{10,11... | collective-permute-start | bytes 1160 | tf_op jit(solution)/shard_map/ppermute | solution.py:70
  42.6 7.7 %collective-permute-start.5 = (bf16[32,128,128]{2,1,0:T(8,128)(2,1)S(1)}, bf16[32,128,128]{2,1,0:T(8,128)(2,1)}, u32[]{:S(2)}, u32[]{:S(2)}) collective-permute-start(bf16[32,128,128]{2,1,0:T(8,128)(2,1)S(1)} %collective-permute-done.2.refs_5_), channel_id=1, source_target_pairs={{0,1},{1,0},{2,3},{3,2},{4,5},{5,4},{6,7},{7,6},{8,9},{9,8},{10,11... | collective-permute-start | bytes 3145736 | tf_op jit(solution)/shard_map/ppermute | solution.py:70
  43.4 6.9 %collective-permute-start.4 = (bf16[32,3,128]{2,1,0:T(4,128)(2,1)S(1)}, bf16[32,3,128]{2,1,0:T(4,128)(2,1)S(1)}, u32[]{:S(2)}, u32[]{:S(2)}) collective-permute-start(bf16[32,3,128]{2,1,0:T(4,128)(2,1)S(1)} %collective-permute-done.1.refs_3_), channel_id=1, source_target_pairs={{0,1},{1,0},{2,3},{3,2},{4,5},{5,4},{6,7},{7,6},{8,9},{9,8},{10,11... | collective-permute-start | bytes 73736 | tf_op jit(solution)/shard_map/ppermute | solution.py:70
  43.7 6.5 %collective-permute-start.3 = (s32[3,32]{1,0:T(4,128)}, s32[3,32]{1,0:T(4,128)S(1)}, u32[]{:S(2)}, u32[]{:S(2)}) collective-permute-start(s32[3,32]{1,0:T(4,128)} %collective-permute-done.refs_1_), channel_id=1, source_target_pairs={{0,1},{1,0},{2,3},{3,2},{4,5},{5,4},{6,7},{7,6},{8,9},{9,8},{10,11... | collective-permute-start | bytes 1160 | tf_op jit(solution)/shard_map/ppermute | solution.py:70

commit v5 on v4

--- a/solution.py
+++ b/solution.py
@@ -449,7 +449,7 @@
     steps = log2(lax.axis_size("dom"))
     sizes = [half >> k for k in range(steps)]
     fold_step = 256
-    lag = 3
+    lag = 4
     turned = turned_units(units)
 
     def kernel(row_ref, back_ref, keep_ref, send_ref, fold_ref, out_ref, *scratch):

time: 95.9 us -> 95.5 us (level)
  no operation moved by 1% of the time
where the time goes in v5:
time: 95.5 us; the launch traced here: 95 us
  Pallas kernels  77.8 us (81%)
  local copies, waits for them, and re-layouts  6.97 us (7%)
  starting transfers between devices  5.17 us (5%)
  other arithmetic  2.99 us (3%)
  between operations  1.42 us (1%)
    pallas_call x1, Pallas kernels, return_and_reduce(): pl.pallas_call(kernel, out_shape=[jax.ShapeDtypeStruct((owned_rows, colum...  36 us
    pallas_call x1, Pallas kernels, element_sums(): pl.pallas_call(kernel, out_shape=[jax.ShapeDtypeStruct((owned_rows, colum...  15.7 us
    pallas_call x1, Pallas kernels, halo_rows(): pl.pallas_call(kernel, out_shape=jax.ShapeDtypeStruct((partitions * width...  13.1 us
    pallas_call x2, Pallas kernels, block_sums(): pl.pallas_call(kernel, out_shape=out_shape, in_specs=[SMEM] * (1 + lists)...  12.9 us
    unnamed x19, local copies, waits for them, and re-layouts  6.12 us
    ppermute x3, starting transfers between devices, shards(): lax.ppermute(value, 'dir', xor_pairs(dir_count, dir_bits - 1))  3.89 us
  transfers between devices with their start and end apart: 9, of which 2 were waited for; matrix products, arithmetic and copies ran while one was open for 3% of the time, Pallas kernels for 23%

profile of v5, /device:TPU:0, one launch (start us, length us, event | category | flops | bytes accessed | tf_op | source)
XLA Modules:
  0.0 95.0 jit_solution(12208833338644523136)
XLA Ops:
  0.6 0.7 copy-done.1
  1.4 1.0 %copy-done.4 = bf16[2048,128]{1,0:T(8,128)(2,1)S(1)} copy-done((bf16[2048,128]{1,0:T(8,128)(2,1)S(1)}, bf16[2048,128]{1,0:T(8,128)(2,1)}, u32[]{:S(2)}) %copy-start.4) | copy-done | bytes 524312
  2.4 13.1 %shard_map.122.halo_ref = bf16[1024,128]{1,0:T(8,128)(2,1)S(1)} custom-call(s32[32,32]{1,0:T(8,128)S(1)} %copy-done.1, bf16[2048,128]{1,0:T(8,128)(2,1)S(1)} %copy-done.4), custom_call_target="tpu_custom_call" | custom-call | flops 1000000000 | bytes 524288 | tf_op jit(solution)/shard_map/pallas_call | solution.py:327
  15.5 0.7 copy-done.7
  16.2 1.8 %collective-permute-start.2 = (bf16[32,128,128]{2,1,0:T(8,128)(2,1)}, bf16[32,128,128]{2,1,0:T(8,128)(2,1)S(1)}, u32[]{:S(2)}, u32[]{:S(2)}) collective-permute-start(bf16[32,128,128]{2,1,0:T(8,128)(2,1)} %refs_5_.1), channel_id=1, source_target_pairs={{0,2},{1,3},{2,0},{3,1},{4,6},{5,7},{6,4},{7,5},{8,10},{9,11},{10,... | collective-permute-start | bytes 3145736 | tf_op jit(solution)/shard_map/ppermute | solution.py:594
  18.0 0.8 copy.13.refs_3_
  18.8 0.3 collective-permute-start.1
  19.1 0.5 collective-permute-start.8
  19.6 0.7 pad_add_fusion.refs_1_
  20.3 1.8 %collective-permute-start = (s32[3,32]{1,0:T(4,128)S(1)}, s32[3,32]{1,0:T(4,128)}, u32[]{:S(2)}, u32[]{:S(2)}) collective-permute-start(s32[3,32]{1,0:T(4,128)S(1)} %pad_add_fusion.refs_1_), channel_id=1, source_target_pairs={{0,2},{1,3},{2,0},{3,1},{4,6},{5,7},{6,4},{7,5},{8,10},{9,11},{10,... | collective-permute-start | bytes 1160 | tf_op jit(solution)/shard_map/ppermute | solution.py:594
  22.1 0.8 reshape.318.link_ref
  23.5 1.0 %copy-done.5 = bf16[2048,128]{1,0:T(8,128)(2,1)S(1)} copy-done((bf16[2048,128]{1,0:T(8,128)(2,1)S(1)}, bf16[2048,128]{1,0:T(8,128)(2,1)}, u32[]{:S(2)}) %copy-start.5) | copy-done | bytes 524312
  24.6 0.9 copy-done.6
  25.5 0.9 copy-done.8
  26.4 15.7 %shard_map.123 = (f32[2048,128]{1,0:T(8,128)S(1)}, bf16[1024,128]{1,0:T(8,128)(2,1)S(1)}) custom-call(s32[6144]{0:T(1024)S(1)} %reshape.318.link_ref, s32[1]{0:T(128)S(6)} %copy.16.live_ref, bf16[2048,128]{1,0:T(8,128)(2,1)S(1)} %copy-done.5, bf16[1024,128]{1,0:T(8,128)(2,1)S(1)} %copy-done.8, f32[36,1024]{1,0:T(8,128)S(1)} %copy-done.6), custom_call_target="tpu_custom_call" | custom-call | flops 4000000000 | bytes 3145728 | tf_op jit(solution)/shard_map/pallas_call | solution.py:422
  42.2 0.4 collective-permute-done.refs_1_
  42.6 0.5 collective-permute-start.5
  43.4 0.3 collective-permute-done.6.refs_2_
  43.7 0.2 collective-permute-start.3
  43.9 6.3 %shard_map.124.refs_7_ = f32[16,512,128]{2,1,0:T(8,128)S(1)} custom-call(f32[3,4]{1,0:T(4,128)S(1)} %copy-done.3, s32[3,32]{1,0:T(4,128)S(1)} %pad_add_fusion.refs_1_, s32[3,32]{1,0:T(4,128)S(1)} %collective-permute-done.6.refs_2_, bf16[32,3,128]{2,1,0:T(4,128)(2,1)S(1)} %copy.13.refs_3_, bf16[32,3,128]{2,1,0:T(4,128)(2,1)S(1)} %collective-permute-done.7.refs_4_, ...), custom_call_target="tpu_custom_call" | custom-call | flops 1073741824 | bytes 6291456 | tf_op jit(solution)/shard_map/pallas_call | solution.py:220
  50.3 6.6 %shard_map.125 = (f32[8,8,64,128]{3,2,1,0:T(8,128)S(1)}, bf16[8,8,64,128]{3,2,1,0:T(8,128)(2,1)S(1)}) custom-call(f32[3,4]{1,0:T(4,128)S(1)} %copy-done.3, s32[3,32]{1,0:T(4,128)} %collective-permute-done.refs_1_, s32[3,32]{1,0:T(4,128)S(1)} %collective-permute-done.3.refs_2_, bf16[32,3,128]{2,1,0:T(4,128)(2,1)S(1)} %collective-permute-done.1.refs_3_, ...), custom_call_target="tpu_custom_call" | custom-call | flops 1073741824 | bytes 6291456 | tf_op jit(solution)/shard_map/pallas_call | solution.py:220
  56.8 36.0 %shard_map.126 = (f32[2048,128]{1,0:T(8,128)S(1)}, f32[2,8,64,128]{3,2,1,0:T(8,128)S(1)}) custom-call(s32[1,1024]{1,0:T(1,128)S(1)} %reshape.319.row_ref, bf16[1024,128]{1,0:T(8,128)(2,1)S(1)} %get-tuple-element.18.back_ref, f32[8,8,64,128]{3,2,1,0:T(8,128)S(1)} %get-tuple-element.22.keep_ref, bf16[8,8,64,128]{3,2,1,0:T(8,128)(2,1)S(1)} %get-tuple-element.23.send_ref), custom_call_target="tpu_custom_call" | custom-call | flops 536870912 | bytes 3145728 | tf_op jit(solution)/shard_map/pallas_call | solution.py:541
  93.0 0.8 pad_maximum_fusion
  93.9 1.1 %add.73 = f32[2048,128]{1,0:T(8,128)} add(f32[2048,128]{1,0:T(8,128)S(1)} %get-tuple-element.15, f32[2048,128]{1,0:T(8,128)S(1)} %get-tuple-element.24) | non-fusion elementwise | flops 262144 | bytes 3145728 | tf_op jit(solution)/shard_map/add | solution.py:603
  (30 shorter events, 0.6 us)
Async XLA Ops:
  0.6 0.7 copy-start.1
  1.3 1.0 %copy-start.4 = (bf16[2048,128]{1,0:T(8,128)(2,1)S(1)}, bf16[2048,128]{1,0:T(8,128)(2,1)}, u32[]{:S(2)}) copy-start(bf16[2048,128]{1,0:T(8,128)(2,1)} %x_ref.3) | copy-start | bytes 1572868
  15.5 0.7 copy-start.7
  16.2 26.3 %collective-permute-start.2 = (bf16[32,128,128]{2,1,0:T(8,128)(2,1)}, bf16[32,128,128]{2,1,0:T(8,128)(2,1)S(1)}, u32[]{:S(2)}, u32[]{:S(2)}) collective-permute-start(bf16[32,128,128]{2,1,0:T(8,128)(2,1)} %refs_5_.1), channel_id=1, source_target_pairs={{0,2},{1,3},{2,0},{3,1},{4,6},{5,7},{6,4},{7,5},{8,10},{9,11},{10,... | collective-permute-start | bytes 3145736 | tf_op jit(solution)/shard_map/ppermute | solution.py:594
  18.8 23.8 %collective-permute-start.1 = (bf16[32,3,128]{2,1,0:T(4,128)(2,1)S(1)}, bf16[32,3,128]{2,1,0:T(4,128)(2,1)S(1)}, u32[]{:S(2)}, u32[]{:S(2)}) collective-permute-start(bf16[32,3,128]{2,1,0:T(4,128)(2,1)S(1)} %copy.13.refs_3_), channel_id=1, source_target_pairs={{0,2},{1,3},{2,0},{3,1},{4,6},{5,7},{6,4},{7,5},{8,10},{9,11},{10,... | collective-permute-start | bytes 73736 | tf_op jit(solution)/shard_map/ppermute | solution.py:594
  19.1 24.8 %collective-permute-start.7 = (bf16[32,3,128]{2,1,0:T(4,128)(2,1)S(1)}, bf16[32,3,128]{2,1,0:T(4,128)(2,1)S(1)}, u32[]{:S(2)}, u32[]{:S(2)}) collective-permute-start(bf16[32,3,128]{2,1,0:T(4,128)(2,1)S(1)} %copy.13.refs_3_), channel_id=1, source_target_pairs={{0,1},{1,0},{2,3},{3,2},{4,5},{5,4},{6,7},{7,6},{8,9},{9,8},{10,11... | collective-permute-start | bytes 73736 | tf_op jit(solution)/shard_map/ppermute | solution.py:70
  19.1 24.8 %collective-permute-start.8 = (bf16[32,128,128]{2,1,0:T(8,128)(2,1)}, bf16[32,128,128]{2,1,0:T(8,128)(2,1)}, u32[]{:S(2)}, u32[]{:S(2)}) collective-permute-start(bf16[32,128,128]{2,1,0:T(8,128)(2,1)} %refs_5_.1), channel_id=1, source_target_pairs={{0,1},{1,0},{2,3},{3,2},{4,5},{5,4},{6,7},{7,6},{8,9},{9,8},{10,11... | collective-permute-start | bytes 3145736 | tf_op jit(solution)/shard_map/ppermute | solution.py:70
  20.3 22.2 %collective-permute-start = (s32[3,32]{1,0:T(4,128)S(1)}, s32[3,32]{1,0:T(4,128)}, u32[]{:S(2)}, u32[]{:S(2)}) collective-permute-start(s32[3,32]{1,0:T(4,128)S(1)} %pad_add_fusion.refs_1_), channel_id=1, source_target_pairs={{0,2},{1,3},{2,0},{3,1},{4,6},{5,7},{6,4},{7,5},{8,10},{9,11},{10,... | collective-permute-start | bytes 1160 | tf_op jit(solution)/shard_map/ppermute | solution.py:594
  23.5 1.0 %copy-start.5 = (bf16[2048,128]{1,0:T(8,128)(2,1)S(1)}, bf16[2048,128]{1,0:T(8,128)(2,1)}, u32[]{:S(2)}) copy-start(bf16[2048,128]{1,0:T(8,128)(2,1)} %x_ref.3) | copy-start | bytes 1572868
  24.6 0.9 copy-start.6
  25.5 0.9 %copy-start.8 = (bf16[1024,128]{1,0:T(8,128)(2,1)S(1)}, bf16[1024,128]{1,0:T(8,128)(2,1)}, u32[]{:S(2)}) copy-start(bf16[1024,128]{1,0:T(8,128)(2,1)} %copy-done.7) | copy-start | bytes 786436
  26.4 16.7 %copy-start.3 = (f32[3,4]{1,0:T(4,128)S(1)}, f32[3,4]{1,0:T(4,128)}, u32[]{:S(2)}) copy-start(f32[3,4]{1,0:T(4,128)} %refs_0_.3) | copy-start | bytes 148
  26.4 16.9 %copy-start.2 = (s32[32,32]{1,0:T(8,128)S(1)}, s32[32,32]{1,0:T(8,128)}, u32[]{:S(2)}) copy-start(s32[32,32]{1,0:T(8,128)} %list_ref.1) | copy-start | bytes 12292
  26.4 17.5 %copy-start = (bf16[32,128,128]{2,1,0:T(8,128)(2,1)S(1)}, bf16[32,128,128]{2,1,0:T(8,128)(2,1)}, u32[]{:S(2)}) copy-start(bf16[32,128,128]{2,1,0:T(8,128)(2,1)} %refs_5_.1) | copy-start | bytes 3145732
  42.5 1.2 %collective-permute-start.6 = (s32[3,32]{1,0:T(4,128)S(1)}, s32[3,32]{1,0:T(4,128)S(1)}, u32[]{:S(2)}, u32[]{:S(2)}) collective-permute-start(s32[3,32]{1,0:T(4,128)S(1)} %pad_add_fusion.refs_1_), channel_id=1, source_target_pairs={{0,1},{1,0},{2,3},{3,2},{4,5},{5,4},{6,7},{7,6},{8,9},{9,8},{10,11... | collective-permute-start | bytes 1160 | tf_op jit(solution)/shard_map/ppermute | solution.py:70
  42.6 7.7 %collective-permute-start.5 = (bf16[32,128,128]{2,1,0:T(8,128)(2,1)S(1)}, bf16[32,128,128]{2,1,0:T(8,128)(2,1)}, u32[]{:S(2)}, u32[]{:S(2)}) collective-permute-start(bf16[32,128,128]{2,1,0:T(8,128)(2,1)S(1)} %collective-permute-done.2.refs_5_), channel_id=1, source_target_pairs={{0,1},{1,0},{2,3},{3,2},{4,5},{5,4},{6,7},{7,6},{8,9},{9,8},{10,11... | collective-permute-start | bytes 3145736 | tf_op jit(solution)/shard_map/ppermute | solution.py:70
  43.4 6.9 %collective-permute-start.4 = (bf16[32,3,128]{2,1,0:T(4,128)(2,1)S(1)}, bf16[32,3,128]{2,1,0:T(4,128)(2,1)S(1)}, u32[]{:S(2)}, u32[]{:S(2)}) collective-permute-start(bf16[32,3,128]{2,1,0:T(4,128)(2,1)S(1)} %collective-permute-done.1.refs_3_), channel_id=1, source_target_pairs={{0,1},{1,0},{2,3},{3,2},{4,5},{5,4},{6,7},{7,6},{8,9},{9,8},{10,11... | collective-permute-start | bytes 73736 | tf_op jit(solution)/shard_map/ppermute | solution.py:70
  43.7 6.5 %collective-permute-start.3 = (s32[3,32]{1,0:T(4,128)}, s32[3,32]{1,0:T(4,128)S(1)}, u32[]{:S(2)}, u32[]{:S(2)}) collective-permute-start(s32[3,32]{1,0:T(4,128)} %collective-permute-done.refs_1_), channel_id=1, source_target_pairs={{0,1},{1,0},{2,3},{3,2},{4,5},{5,4},{6,7},{7,6},{8,9},{9,8},{10,11... | collective-permute-start | bytes 1160 | tf_op jit(solution)/shard_map/ppermute | solution.py:70
